TPU v7x, 512 devices: a whole 4x8x8 slice. The times are simulated.
512 devices in a mesh: paths: 32 (over x, z), trades: 16 (over y, core).
Axes of the slice: x: 4, y: 8, z: 8, core: 2. Of those that a mesh axis runs over, the one named last changes fastest.
Arguments:
- x_train: float32 [8192, 64], P('paths'), may hold values from -6 to 6
- value_label: float32 [8192, 4096], P('paths', 'trades'), may hold values from -6 to 6
- slope_label: float32 [8192, 64], P('paths'), may hold values from -6 to 6
- x_infer: float32 [4, 8192, 64], P(None, 'paths'), may hold values from -6 to 6
- w_in: float32 [64, 512], replicated, may hold values from -0.75 to 0.75
- b_in: float32 [512], replicated, may hold values from -3 to 3
- w_mid: float32 [512, 512], replicated, may hold values from -0.25 to 0.25
- b_mid: float32 [512], replicated, may hold values from -3 to 3
- head: float32 [512, 4096], P(None, 'trades'), may hold values from -0.25 to 0.25
- trade_set: int32 [4096], P('trades'), may hold values from 0 to 255
- trade_sign: int32 [4096], P('trades'), may hold values from 0 to 1
- trade_level: int32 [4096], P('trades'), may hold values from 0 to 7
Outputs:
- grad_w_in: float32 [64, 512], replicated
- grad_b_in: float32 [512], replicated
- grad_w_mid: float32 [512, 512], replicated
- grad_b_mid: float32 [512], replicated
- grad_head: float32 [512, 4096], P(None, 'trades')
- exposure: float32 [4, 256], P(None, 'trades')
All inputs are finite; a program needn't handle non-finite values.
Results may differ from a plain program's by a relative error of at most 0.000061.
Values sent between devices are 32-bit elements; how exact they have to be, the bound alone decides.
No kernel may reach another device: no remote copies, remote signals or barrier semaphores. Data moves between devices by JAX's collectives and lax.ppermute only.
A program may use at most 64 MiB of HBM per device.

v0:
```python
import functools

import jax
import jax.numpy as jnp
from jax import lax
from jax.experimental import pallas as pl
from jax.experimental.pallas import tpu as pltpu
from jax.sharding import Mesh
from jax.sharding import PartitionSpec as P

TRADES = ("trades_0", "trades_1")
F32 = jnp.float32
BF16 = jnp.bfloat16

NN = (((1,), (0,)), ((), ()))
NT = (((1,), (1,)), ((), ()))

VALUE_SCALE = 2.0 / (8192 * 4096)
SLOPE_SCALE = 2.0 / (8192 * 64)
PORT_SCALE = 1.0 / 64.0
LEARN = 0.5

LANE_BMID = 96
LANE_BIN = 104
LANE_PORT = 105
LANE_NET = 112


def halves(a):
    high = a.astype(BF16)
    low = (a - high.astype(F32)).astype(BF16)
    return high, low


def mm(left, right, dims=NN):
    def dot(a, b):
        return lax.dot_general(a, b, dims, preferred_element_type=F32)

    return dot(left[0], right[0]) + (dot(left[0], right[1]) + dot(left[1], right[0]))


def softplus_sigmoid(z):
    e = jnp.exp(-jnp.abs(z))
    act = jnp.maximum(z, 0.0) + jnp.log1p(e)
    slope = jnp.where(z >= 0, 1.0, e) / (1.0 + e)
    return act, slope


def softplus(z):
    return jnp.maximum(z, 0.0) + jnp.log1p(jnp.exp(-jnp.abs(z)))


def trade_weights(sign, level):
    return (2 * sign - 1).astype(F32) * (0.5 + 0.25 * level.astype(F32))


def column_of(row):
    return jnp.broadcast_to(row, (128, row.shape[1])).T[:, 0:1]


def lane_index(shape):
    return lax.broadcasted_iota(jnp.int32, shape, len(shape) - 1)


def forward_kernel(
    x, w_in, b_in, w_mid, b_mid, head, label, sign, level,
    pay, a1_t, s1_t, s2_t, a2_t, dv_t, w_in_t, w_mid_t,
):
    wt = w_in[...].T
    w_in_t[...] = wt
    z1 = mm(halves(wt), halves(x[...]), NT) + column_of(b_in[...])
    a1, s1 = softplus_sigmoid(z1)
    a1_t[...] = a1
    s1_t[...] = s1
    mt = w_mid[...].T
    w_mid_t[...] = mt
    z2 = mm(halves(mt), halves(a1)) + column_of(b_mid[...])
    a2, s2 = softplus_sigmoid(z2)
    a2_t[...] = a2
    s2_t[...] = s2
    hd = head[...]
    hp = halves(hd)
    values = mm(halves(hd.T), halves(a2))
    err = (values - label[...].T) * VALUE_SCALE
    dv_t[...] = err
    d_a2 = mm(hp, halves(err))
    pay[:, 0:32, :] = d_a2[:, 0:128].reshape(16, 32, 128)
    pay[:, 32:64, :] = d_a2[:, 128:256].reshape(16, 32, 128)
    w = trade_weights(sign[...], level[...])
    port = jnp.sum(hd * w, axis=1, keepdims=True)
    for k in range(4):
        col = jnp.broadcast_to(port[128 * k : 128 * k + 128], (128, 128))
        row = col.T[0:1]
        pay[:, 64 + k : 65 + k, :] = jnp.broadcast_to(row[None], (16, 1, 128))
    pay[:, 68:72, :] = jnp.zeros((16, 4, 128), F32)


def head_grad_kernel(a2_t, dv_t, out):
    out[...] = mm(halves(a2_t[...]), halves(dv_t[...]), NT)


def backward_kernel(
    own, arrived, x, slope_label_t, w_in, w_in_t, w_mid, w_mid_t, a1_t, s1_t, s2_t, g_head,
    pay, u2_s, q_s, z_s,
):
    rows = pl.ds(pl.multiple_of(own[0] * 32, 32), 32)
    total = jnp.sum(arrived[...], axis=0)
    d_a2 = jnp.concatenate([total[0:32], total[32:64]], axis=1)
    port = jnp.concatenate(
        [column_of(total[64 + k : 65 + k]) for k in range(4)], axis=0
    ) * PORT_SCALE
    s1 = s1_t[...]
    s2 = s2_t[...]
    u2 = port * s2
    u2_s[...] = u2
    v1 = mm(halves(w_mid[...]), halves(u2))
    u1 = v1 * s1
    slopes = mm(halves(w_in[...]), halves(u1))
    d_slope = (slopes - slope_label_t[...]) * SLOPE_SCALE
    du1 = mm(halves(w_in_t[...]), halves(d_slope))
    dv1 = du1 * s1
    ds1 = du1 * v1
    dv1_p = halves(dv1)
    du2 = mm(halves(w_mid_t[...]), dv1_p)
    du2_s2 = du2 * s2
    g_port = jnp.sum(du2_s2, axis=1, keepdims=True)
    q_s[...] = du2_s2 * port * (1.0 - s2)
    dz2 = d_a2 * s2_t[rows, :] + q_s[rows, :]
    z_s[...] = jnp.zeros_like(z_s)
    z_s[rows, :] = dz2
    da1 = mm(halves(w_mid[...]), halves(z_s[...]))
    dz1 = da1 * s1 + (ds1 * s1 * (1.0 - s1)) * (1.0 / 16.0)
    g_b_in = jnp.sum(dz1, axis=1, keepdims=True)
    none = jnp.zeros((64, 256), F32)
    few = jnp.zeros((32, 256), F32)
    mid_a = jnp.concatenate([none, dz2, few], axis=0)
    mid_b = jnp.concatenate([none, u2_s[rows, :], few], axis=0)
    slope_rows = jnp.concatenate([d_slope * (1.0 / 16.0), none], axis=0)
    x_t = jnp.concatenate([x[...].T, none], axis=0)
    ext = mm(halves(a1_t[...]), halves(mid_a), NT)
    ext = ext + mm(dv1_p, halves(mid_b), NT)
    ext = ext + mm(halves(u1), halves(slope_rows), NT)
    ext = ext + mm(halves(dz1), halves(x_t), NT)
    lane = lane_index((512, 128))
    ext = jnp.where(lane == LANE_BIN, g_b_in, ext)
    ext = jnp.where(lane == LANE_PORT, g_port, ext)
    b_mid = jnp.sum(dz2, axis=1, keepdims=True)
    unit = lax.broadcasted_iota(jnp.int32, (32, 128), 0)
    spot = lane_index((32, 128)) == LANE_BMID + (unit & 7)
    spread = jnp.where(spot, b_mid, 0.0)
    lines = [jnp.sum(spread[8 * k : 8 * k + 8], axis=0, keepdims=True) for k in range(4)]
    tile = jnp.concatenate(lines + [jnp.zeros((4, 128), F32)], axis=0)
    blocks = ext.reshape(64, 8, 128) + tile[None]
    pay[:, 0:8, :] = blocks[0:32]
    pay[:, 8:16, :] = blocks[32:64]
    pay[:, 16:24, :] = g_head[0:256, 0:128].reshape(32, 8, 128)
    pay[:, 24:32, :] = g_head[0:256, 128:256].reshape(32, 8, 128)
    pay[:, 32:40, :] = g_head[256:512, 0:128].reshape(32, 8, 128)
    pay[:, 40:48, :] = g_head[256:512, 128:256].reshape(32, 8, 128)


def net_kernel(own, arrived, head, sets, sign, level, pay, head_shard):
    total = jnp.sum(arrived[...], axis=0)
    trunk = total[0:16]
    w = trade_weights(sign[...], level[...])
    upper = jnp.concatenate([total[16:24], total[24:32]], axis=1)
    lower = jnp.concatenate([total[32:40], total[40:48]], axis=1)
    g_head = jnp.concatenate([upper, lower], axis=0)
    g_head = g_head + trunk[:, LANE_PORT : LANE_PORT + 1] * (w * PORT_SCALE)
    head_shard[0:8, :] = g_head[0:8, 0:128]
    head_shard[8:16, :] = g_head[0:8, 128:256]
    head_shard[16:24, :] = g_head[8:16, 0:128]
    head_shard[24:32, :] = g_head[8:16, 128:256]
    first = pl.multiple_of(own[0] * 8, 8)
    second = pl.multiple_of(own[0] * 8 + 256, 8)
    old = jnp.concatenate([head[pl.ds(first, 8), :], head[pl.ds(second, 8), :]], axis=0)
    weighted = halves((old - LEARN * g_head) * w)
    ids = jnp.broadcast_to(sets[...], (128, 256))
    place = lax.broadcasted_iota(jnp.int32, (128, 256), 0) - LANE_NET
    lane = lane_index((16, 128))
    for t in range(16):
        member = ((ids == place + 16 * t) & (place >= 0)).astype(F32).astype(BF16)
        net = lax.dot_general(weighted[0], member, NT, preferred_element_type=F32)
        net = net + lax.dot_general(weighted[1], member, NT, preferred_element_type=F32)
        pay[t] = jnp.where(lane < LANE_NET, trunk, net)


def gather_kernel(core, arrived, pay, g_b_mid):
    total = jnp.sum(arrived[...], axis=0)
    lane = lane_index((16, 128))
    row_lane = lane_index((1, 128))
    first = core[0] == 0
    tiles = []
    for k in range(4):
        block = jnp.zeros((16, 128), F32)
        bias = jnp.zeros((1, 128), F32)
        for m in range(4):
            part = arrived[4 * k + m]
            moved = part if m == 2 else pltpu.roll(part, (32 * m - 64) % 128, 1)
            block = jnp.where((lane >= 32 * m) & (lane < 32 * m + 32), moved, block)
            for r in range(4):
                to = 32 * m + 8 * r
                shift = (to - LANE_BMID) % 128
                line = part[0:8] if shift == 0 else pltpu.roll(part[0:8], shift, 1)
                bias = jnp.where((row_lane >= to) & (row_lane < to + 8), line[r : r + 1], bias)
        g_b_mid[:, 128 * k : 128 * k + 128] = bias
        tiles.append(jnp.where(first, block[0:8], block[8:16]))
    packed = jnp.concatenate(tiles + [total], axis=0)
    pay[...] = jnp.broadcast_to(packed[None], (32, 48, 128))


def infer_kernel(
    core, mine, other, w_in, b_in, w_mid, b_mid, g_b_mid, x, head_shard,
    g_in_out, g_b_in_out, g_mid_out, pay,
):
    first = core[0] == 0
    for k in range(4):
        a = mine[:, 8 * k : 8 * k + 8, :].reshape(256, 128)
        b = other[:, 8 * k : 8 * k + 8, :].reshape(256, 128)
        g_mid_out[0:256, 128 * k : 128 * k + 128] = jnp.where(first, a, b)
        g_mid_out[256:512, 128 * k : 128 * k + 128] = jnp.where(first, b, a)
    upper = mine[:, 32:40, :].reshape(256, 128)
    lower = mine[:, 40:48, :].reshape(256, 128)
    both = jnp.concatenate([upper, lower], axis=0)
    flat = both.T
    g_in = flat[0:64]
    g_b_in = flat[LANE_BIN : LANE_BIN + 1]
    g_in_out[...] = g_in
    g_b_in_out[...] = g_b_in
    new_in = halves(w_in[...] - LEARN * g_in)
    new_b_in = b_in[...] - LEARN * g_b_in
    new_mid = halves(w_mid[...] - LEARN * g_mid_out[...])
    new_b_mid = b_mid[...] - LEARN * g_b_mid[...]
    net_head = halves(both)
    sums = []
    for d in range(4):
        a1 = softplus(mm(halves(x[d]), new_in) + new_b_in)
        a2 = softplus(mm(halves(a1), new_mid) + new_b_mid)
        netted = mm(halves(a2), net_head)
        sums.append(jnp.sum(jnp.maximum(netted, 0.0), axis=0, keepdims=True))
    tile = jnp.concatenate(sums + [jnp.zeros((4, 128), F32)], axis=0)
    pay[:, 0:32, :] = jnp.broadcast_to(head_shard[...][None], (32, 32, 128))
    pay[:, 32:40, :] = jnp.broadcast_to(tile[None], (32, 8, 128))


def finish_kernel(arrived, g_head, exposure):
    g_head[0:256, 0:128] = arrived[:, 0:8, :].reshape(256, 128)
    g_head[0:256, 128:256] = arrived[:, 8:16, :].reshape(256, 128)
    g_head[256:512, 0:128] = arrived[:, 16:24, :].reshape(256, 128)
    g_head[256:512, 128:256] = arrived[:, 24:32, :].reshape(256, 128)
    total = jnp.sum(arrived[:, 32:40, :], axis=0) * (1.0 / 8192.0)
    moved = pltpu.roll(total, 128 - LANE_NET, 1)
    exposure[...] = moved[0:4, 0:16]


def call(kernel, outs, scalars, args, scratch=(), flops=0):
    shapes = tuple(jax.ShapeDtypeStruct(s, F32) for s in outs)
    vmem = pl.BlockSpec(memory_space=pltpu.VMEM)
    smem = pl.BlockSpec(memory_space=pltpu.SMEM)
    return pl.pallas_call(
        kernel,
        out_shape=shapes,
        in_specs=[smem] * len(scalars) + [vmem] * len(args),
        out_specs=tuple(vmem for _ in outs),
        scratch_shapes=[pltpu.VMEM(s, F32) for s in scratch],
        cost_estimate=pl.CostEstimate(flops=flops, transcendentals=0, bytes_accessed=0),
        name=kernel.__name__,
    )(*scalars, *args)


def swap(x, axis):
    return lax.all_to_all(x, axis, 0, 0, tiled=True)


def on_device(
    x_train, value_label, slope_label, x_infer, w_in, b_in, w_mid, b_mid, head,
    trade_set, trade_sign, trade_level,
):
    path = lax.axis_index("paths").astype(jnp.int32).reshape(1)
    trade = lax.axis_index(TRADES).astype(jnp.int32).reshape(1)
    core = lax.axis_index("trades_1").astype(jnp.int32).reshape(1)
    b_in_r = b_in.reshape(1, -1)
    b_mid_r = b_mid.reshape(1, -1)
    sets = trade_set.reshape(1, -1)
    sign = trade_sign.reshape(1, -1)
    level = trade_level.reshape(1, -1)
    act = (512, 256)
    pay1, a1_t, s1_t, s2_t, a2_t, dv_t, w_in_t, w_mid_t = call(
        forward_kernel,
        [(16, 72, 128), act, act, act, act, (256, 256), (512, 64), (512, 512)],
        [],
        [x_train, w_in, b_in_r, w_mid, b_mid_r, head, value_label, sign, level],
        flops=10**9,
    )
    arr1 = swap(pay1, TRADES)
    (g_head,) = call(head_grad_kernel, [act], [], [a2_t, dv_t], flops=4 * 10**8)
    (pay2,) = call(
        backward_kernel,
        [(32, 48, 128)],
        [trade],
        [arr1, x_train, slope_label.T, w_in, w_in_t, w_mid, w_mid_t, a1_t, s1_t, s2_t, g_head],
        scratch=[act, act, act],
        flops=10**9,
    )
    arr2 = swap(pay2, "paths")
    pay3, head_shard = call(
        net_kernel,
        [(16, 16, 128), (32, 128)],
        [path],
        [arr2, head, sets, sign, level],
        flops=10**8,
    )
    arr3 = swap(pay3, TRADES)
    pay4, g_b_mid = call(gather_kernel, [(32, 48, 128), (1, 512)], [core], [arr3], flops=10**8)
    mine = swap(pay4, "paths")
    other = lax.ppermute(mine, "trades_1", [(0, 1), (1, 0)])
    g_in, g_b_in, g_mid, pay6 = call(
        infer_kernel,
        [(64, 512), (1, 512), (512, 512), (32, 40, 128)],
        [core],
        [mine, other, w_in, b_in_r, w_mid, b_mid_r, g_b_mid, x_infer, head_shard],
        flops=10**9,
    )
    arr6 = swap(pay6, "paths")
    g_head_all, exposure = call(finish_kernel, [act, (4, 16)], [], [arr6], flops=10**6)
    return (g_in, g_b_in.reshape(-1), g_mid, g_b_mid.reshape(-1), g_head_all, exposure)


def solution(mesh):
    torus = Mesh(mesh.devices.reshape(mesh.shape["paths"], 8, 2), ("paths", "trades_0", "trades_1"))
    return jax.shard_map(
        on_device,
        mesh=torus,
        in_specs=(
            P("paths", None),
            P("paths", TRADES),
            P("paths", None),
            P(None, "paths", None),
            P(),
            P(),
            P(),
            P(),
            P(None, TRADES),
            P(TRADES),
            P(TRADES),
            P(TRADES),
        ),
        out_specs=(P(), P(), P(), P(), P(None, TRADES), P(None, TRADES)),
        check_vma=False,
    )
```

profile of v0, /device:TPU:1, one launch (start us, length us, event | category | flops | bytes accessed | tf_op | source)
XLA Modules:
  0.0 164.0 jit_solution(17637315496756931740)
XLA Ops:
  0.6 1.6 copy.18.x
  2.2 5.2 %forward_kernel.1 = (f32[16,72,128]{2,1,0:T(8,128)}, f32[512,256]{1,0:T(8,128)}, f32[512,256]{1,0:T(8,128)}, f32[512,256]{1,0:T(8,128)}, f32[512,256]{1,0:T(8,12...) custom-call(f32[256,64]{1,0:T(8,128)} %copy.18.x, f32[64,512]{1,0:T(8,128)} %w_in.5, ...), custom_call_target="tpu_custom_call" | custom-call | flops 1000000000 | tf_op jit(solution)/shard_map/forward_kernel/pallas_call | solution.py:260
  7.5 10.2 %all-to-all-start = ((f32[16,72,128]{2,1,0:T(8,128)}), f32[16,72,128]{2,1,0:T(8,128)S(1)}, u32[]{:S(2)}, u32[]{:S(2)}) async-start(f32[16,72,128]{2,1,0:T(8,128)} %get-tuple-element.24), calls=%async_computation | async-start | bytes 1179648 | tf_op jit(solution)/shard_map/all_to_all | solution.py:272
  17.7 2.3 %head_grad_kernel.1.g_head = f32[512,256]{1,0:T(8,128)} custom-call(f32[512,256]{1,0:T(8,128)} %get-tuple-element.30.a2_t, f32[256,256]{1,0:T(8,128)} %get-tuple-element.31.dv_t), custom_call_target="tpu_custom_call" | custom-call | flops 400000000 | tf_op jit(solution)/shard_map/head_grad_kernel/pallas_call | solution.py:260
  20.0 16.4 %all-to-all-done.arrived = f32[16,72,128]{2,1,0:T(8,128)S(1)} async-done(((f32[16,72,128]{2,1,0:T(8,128)}), f32[16,72,128]{2,1,0:T(8,128)S(1)}, u32[]{:S(2)}, u32[]{:S(2)}) %all-to-all-start) | async-done | bytes 589856 | tf_op jit(solution)/shard_map/all_to_all | solution.py:272
  36.4 0.0 copy-start.1
  36.4 0.8 copy-done.1
  37.2 7.6 %backward_kernel.1 = f32[32,48,128]{2,1,0:T(8,128)} custom-call(s32[1]{0:T(128)} %bitcast.2.own, f32[16,72,128]{2,1,0:T(8,128)} %copy-done.1, f32[256,64]{1,0:T(8,128)} %copy.18.x, f32[64,256]{1,0:T(8,128)} %bitcast.11, f32[64,512]{1,0:T(8,128)} %w_in.5, f32[512,64]{1,0:T(8,128)} %get-tuple-element.25.w_in_t, f32[512,512]{1,0:T(8,128)} %w_mid.5, ...), custom_call_target="tpu_custom_call" | custom-call | flops 1000000000 | tf_op jit(solution)/shard_map/backward_kernel/pallas_call | solution.py:260
  44.9 11.1 %all-to-all-start.1 = ((f32[32,48,128]{2,1,0:T(8,128)}), f32[32,48,128]{2,1,0:T(8,128)S(1)}, u32[]{:S(2)}, u32[]{:S(2)}) async-start(f32[32,48,128]{2,1,0:T(8,128)} %backward_kernel.1), calls=%async_computation.1 | async-start | bytes 1572864 | tf_op jit(solution)/shard_map/all_to_all | solution.py:272
  56.0 22.4 %all-to-all-done.1.arrived = f32[32,48,128]{2,1,0:T(8,128)S(1)} async-done(((f32[32,48,128]{2,1,0:T(8,128)}), f32[32,48,128]{2,1,0:T(8,128)S(1)}, u32[]{:S(2)}, u32[]{:S(2)}) %all-to-all-start.1) | async-done | bytes 786464 | tf_op jit(solution)/shard_map/all_to_all | solution.py:272
  78.4 0.0 copy-start
  78.4 0.9 copy-done
  79.3 2.7 %net_kernel.1 = (f32[16,16,128]{2,1,0:T(8,128)}, f32[32,128]{1,0:T(8,128)}) custom-call(s32[1]{0:T(128)} %bitcast.1.own, f32[32,48,128]{2,1,0:T(8,128)} %copy-done, f32[512,256]{1,0:T(8,128)} %head.3, s32[1,256]{1,0:T(1,128)} %bitcast.16, s32[1,256]{1,0:T(1,128)} %bitcast.13, s32[1,256]{1,0:T(1,128)} %bitcast.15), custom_call_target="tpu_custom_call" | custom-call | flops 100000000 | tf_op jit(solution)/shard_map/net_kernel/pallas_call | solution.py:260
  82.0 12.8 %all_to_all.25.arrived = f32[16,16,128]{2,1,0:T(8,128)} all-to-all(f32[16,16,128]{2,1,0:T(8,128)} %get-tuple-element.32), channel_id=1, replica_groups=mesh['paths'=32,'trades_0'=8,'trades_1'=2] {'trades_0','trades_1'}, dimensions={0} | all-to-all | bytes 262144 | tf_op jit(solution)/shard_map/all_to_all | solution.py:272
  94.8 2.0 %gather_kernel.1 = (f32[32,48,128]{2,1,0:T(8,128)}, f32[1,512]{1,0:T(1,128)}) custom-call(s32[1]{0:T(128)} %bitcast.core, f32[16,16,128]{2,1,0:T(8,128)} %all_to_all.25.arrived), custom_call_target="tpu_custom_call" | custom-call | flops 100000000 | tf_op jit(solution)/shard_map/gather_kernel/pallas_call | solution.py:260
  96.8 0.0 copy-start.3
  96.8 27.6 %all_to_all.26.mine = f32[32,48,128]{2,1,0:T(8,128)S(1)} all-to-all(f32[32,48,128]{2,1,0:T(8,128)} %get-tuple-element.33), channel_id=1, replica_groups=mesh['paths'=32,'trades_0'=8,'trades_1'=2] {'paths'}, dimensions={0} | all-to-all | bytes 1572864 | tf_op jit(solution)/shard_map/all_to_all | solution.py:272
  124.3 0.0 copy-start.2
  124.3 3.7 %collective-permute-start = (f32[32,48,128]{2,1,0:T(8,128)S(1)}, f32[32,48,128]{2,1,0:T(8,128)S(1)}, u32[]{:S(2)}, u32[]{:S(2)}) collective-permute-start(f32[32,48,128]{2,1,0:T(8,128)S(1)} %all_to_all.26.mine), channel_id=1, source_target_pairs={{0,1},{1,0},{2,3},{3,2},{4,5},{5,4},{6,7},{7,6},{8,9},{9,8},{10,11... | collective-permute-start | bytes 2359304 | tf_op jit(solution)/shard_map/ppermute | solution.py:316
  128.1 0.0 copy-done.3
  128.1 1.0 copy.20.x
  129.1 0.7 collective-permute-done.other
  129.8 0.0 copy-start.4
  129.8 0.0 copy-done.2
  129.8 0.9 copy-done.4
  130.7 8.9 %infer_kernel.1 = (f32[64,512]{1,0:T(8,128)}, f32[1,512]{1,0:T(1,128)}, f32[512,512]{1,0:T(8,128)}, f32[32,40,128]{2,1,0:T(8,128)}) custom-call(s32[1]{0:T(128)} %bitcast.core, f32[32,48,128]{2,1,0:T(8,128)} %copy-done.2, f32[32,48,128]{2,1,0:T(8,128)} %copy-done.4, f32[64,512]{1,0:T(8,128)} %w_in.5, f32[1,512]{1,0:T(1,128)} %bitcast.18, f32[512,512]{1,0:T(8,128)} %w_mid.5, ...), custom_call_target="tpu_custom_call" | custom-call | flops 1000000000 | tf_op jit(solution)/shard_map/infer_kernel/pallas_call | solution.py:260
  139.6 22.5 %all_to_all.27.arrived = f32[32,40,128]{2,1,0:T(8,128)} all-to-all(f32[32,40,128]{2,1,0:T(8,128)} %get-tuple-element.39), channel_id=1, replica_groups=mesh['paths'=32,'trades_0'=8,'trades_1'=2] {'paths'}, dimensions={0} | all-to-all | bytes 1310720 | tf_op jit(solution)/shard_map/all_to_all | solution.py:272
  162.1 1.9 %finish_kernel.1 = (f32[512,256]{1,0:T(8,128)}, f32[4,16]{1,0:T(4,128)}) custom-call(f32[32,40,128]{2,1,0:T(8,128)} %all_to_all.27.arrived), custom_call_target="tpu_custom_call" | custom-call | flops 1000000 | tf_op jit(solution)/shard_map/finish_kernel/pallas_call | solution.py:260
Async XLA Ops:
  7.5 28.9 %all-to-all-start = ((f32[16,72,128]{2,1,0:T(8,128)}), f32[16,72,128]{2,1,0:T(8,128)S(1)}, u32[]{:S(2)}, u32[]{:S(2)}) async-start(f32[16,72,128]{2,1,0:T(8,128)} %get-tuple-element.24), calls=%async_computation | async-start | bytes 1179648 | tf_op jit(solution)/shard_map/all_to_all | solution.py:272
  36.4 0.8 copy-start.1
  44.9 33.6 %all-to-all-start.1 = ((f32[32,48,128]{2,1,0:T(8,128)}), f32[32,48,128]{2,1,0:T(8,128)S(1)}, u32[]{:S(2)}, u32[]{:S(2)}) async-start(f32[32,48,128]{2,1,0:T(8,128)} %backward_kernel.1), calls=%async_computation.1 | async-start | bytes 1572864 | tf_op jit(solution)/shard_map/all_to_all | solution.py:272
  78.4 0.9 copy-start
  96.8 31.3 %copy-start.3 = (f32[4,256,64]{1,2,0:T(8,128)S(1)}, f32[4,256,64]{1,2,0:T(8,128)}, u32[]{:S(2)}) copy-start(f32[4,256,64]{1,2,0:T(8,128)} %param.15) | copy-start | bytes 786436
  124.3 5.4 %copy-start.2 = (f32[32,48,128]{2,1,0:T(8,128)}, f32[32,48,128]{2,1,0:T(8,128)S(1)}, u32[]{:S(2)}) copy-start(f32[32,48,128]{2,1,0:T(8,128)S(1)} %all_to_all.26.mine) | copy-start | bytes 2359300
  124.3 5.4 %collective-permute-start = (f32[32,48,128]{2,1,0:T(8,128)S(1)}, f32[32,48,128]{2,1,0:T(8,128)S(1)}, u32[]{:S(2)}, u32[]{:S(2)}) collective-permute-start(f32[32,48,128]{2,1,0:T(8,128)S(1)} %all_to_all.26.mine), channel_id=1, source_target_pairs={{0,1},{1,0},{2,3},{3,2},{4,5},{5,4},{6,7},{7,6},{8,9},{9,8},{10,11... | collective-permute-start | bytes 2359304 | tf_op jit(solution)/shard_map/ppermute | solution.py:316
  129.8 0.9 copy-start.4
where the time goes:
time: 167 us; the launch traced here: 164 us
  blocking collectives  62.8 us (38%)
  waiting for transfers between devices  39.5 us (24%)
  Pallas kernels  30.7 us (18%)
  starting transfers between devices  25.1 us (15%)
  local copies, waits for them, and re-layouts  5.23 us (3%)
    all_to_all x3, blocking collectives, swap(): return lax.all_to_all(x, axis, 0, 0, tiled=True)  62.8 us
    all_to_all x2, waiting for transfers between devices, swap(): return lax.all_to_all(x, axis, 0, 0, tiled=True)  38.8 us
    pallas_call x7, Pallas kernels, call(): pl.pallas_call(kernel, out_shape=shapes, in_specs=[smem] * len(scalars) +...  30.7 us
    all_to_all x2, starting transfers between devices, swap(): return lax.all_to_all(x, axis, 0, 0, tiled=True)  21.3 us
    unnamed x12, local copies, waits for them, and re-layouts  5.23 us
    ppermute x1, starting transfers between devices, on_device(): other = lax.ppermute(mine, 'trades_1', [(0, 1), (1, 0)])  3.71 us
  transfers between devices with their start and end apart: 3, of which 3 were waited for; matrix products, arithmetic and copies ran while one was open for 1% of the time, Pallas kernels for 1%

commit v1 on v0

--- a/solution.py
+++ b/solution.py
@@ -24,6 +24,8 @@
 LANE_BIN = 104
 LANE_PORT = 105
 LANE_NET = 112
+LANE_NET_UPPER = 96
+LANE_BIN_LATE = 64
 
 
 def halves(a):
@@ -63,12 +65,12 @@
 
 
 def forward_kernel(
-    x, w_in, b_in, w_mid, b_mid, head, label, sign, level,
+    path, trade, core, x_t, w_in, b_in, w_mid, b_mid, head, label, sign, level,
     pay, a1_t, s1_t, s2_t, a2_t, dv_t, w_in_t, w_mid_t,
 ):
     wt = w_in[...].T
     w_in_t[...] = wt
-    z1 = mm(halves(wt), halves(x[...]), NT) + column_of(b_in[...])
+    z1 = mm(halves(wt), halves(x_t[...])) + column_of(b_in[...])
     a1, s1 = softplus_sigmoid(z1)
     a1_t[...] = a1
     s1_t[...] = s1
@@ -100,7 +102,7 @@
 
 
 def backward_kernel(
-    own, arrived, x, slope_label_t, w_in, w_in_t, w_mid, w_mid_t, a1_t, s1_t, s2_t, g_head,
+    own, arrived, x_t, slope_label_t, w_in, w_in_t, w_mid, w_mid_t, a1_t, s1_t, s2_t, g_head,
     pay, u2_s, q_s, z_s,
 ):
     rows = pl.ds(pl.multiple_of(own[0] * 32, 32), 32)
@@ -136,11 +138,11 @@
     mid_a = jnp.concatenate([none, dz2, few], axis=0)
     mid_b = jnp.concatenate([none, u2_s[rows, :], few], axis=0)
     slope_rows = jnp.concatenate([d_slope * (1.0 / 16.0), none], axis=0)
-    x_t = jnp.concatenate([x[...].T, none], axis=0)
+    x_rows = jnp.concatenate([x_t[...], none], axis=0)
     ext = mm(halves(a1_t[...]), halves(mid_a), NT)
     ext = ext + mm(dv1_p, halves(mid_b), NT)
     ext = ext + mm(halves(u1), halves(slope_rows), NT)
-    ext = ext + mm(halves(dz1), halves(x_t), NT)
+    ext = ext + mm(halves(dz1), halves(x_rows), NT)
     lane = lane_index((512, 128))
     ext = jnp.where(lane == LANE_BIN, g_b_in, ext)
     ext = jnp.where(lane == LANE_PORT, g_port, ext)
@@ -185,11 +187,11 @@
         pay[t] = jnp.where(lane < LANE_NET, trunk, net)
 
 
-def gather_kernel(core, arrived, pay, g_b_mid):
+def gather_kernel(own, arrived, pay, g_b_mid):
     total = jnp.sum(arrived[...], axis=0)
     lane = lane_index((16, 128))
     row_lane = lane_index((1, 128))
-    first = core[0] == 0
+    first = own[0] == 0
     tiles = []
     for k in range(4):
         block = jnp.zeros((16, 128), F32)
@@ -205,26 +207,37 @@
                 bias = jnp.where((row_lane >= to) & (row_lane < to + 8), line[r : r + 1], bias)
         g_b_mid[:, 128 * k : 128 * k + 128] = bias
         tiles.append(jnp.where(first, block[0:8], block[8:16]))
-    packed = jnp.concatenate(tiles + [total], axis=0)
-    pay[...] = jnp.broadcast_to(packed[None], (32, 48, 128))
+    upper, lower = total[0:8], total[8:16]
+    own_rows = jnp.where(first, upper, lower)
+    net_shift = (LANE_NET_UPPER - LANE_NET) % 128
+    eight = lane_index((8, 128))
+    bias_rows = pltpu.roll(own_rows, (LANE_BIN_LATE - LANE_BIN) % 128, 1)
+    own_rows = jnp.where(eight < LANE_BIN_LATE, own_rows, bias_rows)
+    mixed = jnp.where(eight < LANE_NET_UPPER, own_rows, pltpu.roll(upper, net_shift, 1))
+    mixed = jnp.where(eight < LANE_NET, mixed, lower)
+    packed = jnp.concatenate(tiles + [mixed], axis=0)
+    pay[...] = jnp.broadcast_to(packed[None], (32, 40, 128))
 
 
 def infer_kernel(
-    core, mine, other, w_in, b_in, w_mid, b_mid, g_b_mid, x, head_shard,
+    own, mine, other, w_in, b_in, w_mid, b_mid, g_b_mid, x_t, head_shard,
     g_in_out, g_b_in_out, g_mid_out, pay,
 ):
-    first = core[0] == 0
+    first = own[0] == 0
     for k in range(4):
         a = mine[:, 8 * k : 8 * k + 8, :].reshape(256, 128)
         b = other[:, 8 * k : 8 * k + 8, :].reshape(256, 128)
         g_mid_out[0:256, 128 * k : 128 * k + 128] = jnp.where(first, a, b)
         g_mid_out[256:512, 128 * k : 128 * k + 128] = jnp.where(first, b, a)
-    upper = mine[:, 32:40, :].reshape(256, 128)
-    lower = mine[:, 40:48, :].reshape(256, 128)
-    both = jnp.concatenate([upper, lower], axis=0)
-    flat = both.T
+    near = mine[:, 32:40, :].reshape(256, 128)
+    away = other[:, 32:40, :].reshape(256, 128)
+    upper = jnp.where(first, near, away)
+    lower = jnp.where(first, away, near)
+    flat = jnp.concatenate([upper, lower], axis=0).T
     g_in = flat[0:64]
-    g_b_in = flat[LANE_BIN : LANE_BIN + 1]
+    g_b_in = flat[LANE_BIN_LATE : LANE_BIN_LATE + 1]
+    net_shift = (LANE_NET - LANE_NET_UPPER) % 128
+    both = jnp.concatenate([pltpu.roll(near, net_shift, 1), near], axis=0)
     g_in_out[...] = g_in
     g_b_in_out[...] = g_b_in
     new_in = halves(w_in[...] - LEARN * g_in)
@@ -234,7 +247,7 @@
     net_head = halves(both)
     sums = []
     for d in range(4):
-        a1 = softplus(mm(halves(x[d]), new_in) + new_b_in)
+        a1 = softplus(mm(halves(x_t[d].T), new_in) + new_b_in)
         a2 = softplus(mm(halves(a1), new_mid) + new_b_mid)
         netted = mm(halves(a2), net_head)
         sums.append(jnp.sum(jnp.maximum(netted, 0.0), axis=0, keepdims=True))
@@ -253,10 +266,23 @@
     exposure[...] = moved[0:4, 0:16]
 
 
-def call(kernel, outs, scalars, args, scratch=(), flops=0):
-    shapes = tuple(jax.ShapeDtypeStruct(s, F32) for s in outs)
+def keep(a):
+    return pltpu.with_memory_space_constraint(a, pltpu.VMEM)
+
+
+def far(a):
+    return pltpu.with_memory_space_constraint(a, pltpu.HBM)
+
+
+def call(kernel, outs, scalars, args, scratch=(), flops=0, placed=(), final=(), away=()):
+    shapes = tuple(
+        pltpu.HBM(s, F32) if i in final else pltpu.VMEM(s, F32)
+        for i, s in enumerate(outs)
+    )
     vmem = pl.BlockSpec(memory_space=pltpu.VMEM)
     smem = pl.BlockSpec(memory_space=pltpu.SMEM)
+    args = [keep(a) if any(a is p for p in placed) else a for a in args]
+    args = [far(a) if any(a is p for p in away) else a for a in args]
     return pl.pallas_call(
         kernel,
         out_shape=shapes,
@@ -264,6 +290,7 @@
         out_specs=tuple(vmem for _ in outs),
         scratch_shapes=[pltpu.VMEM(s, F32) for s in scratch],
         cost_estimate=pl.CostEstimate(flops=flops, transcendentals=0, bytes_accessed=0),
+        compiler_params=pltpu.CompilerParams(vmem_limit_bytes=24 * 2**20),
         name=kernel.__name__,
     )(*scalars, *args)
 
@@ -285,22 +312,29 @@
     sign = trade_sign.reshape(1, -1)
     level = trade_level.reshape(1, -1)
     act = (512, 256)
+    x_t = x_train.T
+    slope_label_t = slope_label.T
+    x_infer_t = x_infer.transpose(0, 2, 1)
     pay1, a1_t, s1_t, s2_t, a2_t, dv_t, w_in_t, w_mid_t = call(
         forward_kernel,
         [(16, 72, 128), act, act, act, act, (256, 256), (512, 64), (512, 512)],
-        [],
-        [x_train, w_in, b_in_r, w_mid, b_mid_r, head, value_label, sign, level],
+        [path, trade, core],
+        [x_t, w_in, b_in_r, w_mid, b_mid_r, head, value_label, sign, level],
         flops=10**9,
+        final=(0, 2, 3, 4, 5),
+        away=[x_t, w_in, w_mid, head, value_label, b_in_r, b_mid_r, sign, level],
     )
     arr1 = swap(pay1, TRADES)
-    (g_head,) = call(head_grad_kernel, [act], [], [a2_t, dv_t], flops=4 * 10**8)
+    (g_head,) = call(head_grad_kernel, [act], [], [a2_t, dv_t], flops=4 * 10**8, final=(0,), away=[a2_t, dv_t])
     (pay2,) = call(
         backward_kernel,
         [(32, 48, 128)],
         [trade],
-        [arr1, x_train, slope_label.T, w_in, w_in_t, w_mid, w_mid_t, a1_t, s1_t, s2_t, g_head],
+        [arr1, x_t, slope_label_t, w_in, w_in_t, w_mid, w_mid_t, a1_t, s1_t, s2_t, g_head],
         scratch=[act, act, act],
         flops=10**9,
+        placed=[arr1, w_in_t, w_mid_t, a1_t, w_mid],
+        away=[s1_t, s2_t, g_head, x_t, slope_label_t, w_in],
     )
     arr2 = swap(pay2, "paths")
     pay3, head_shard = call(
@@ -309,20 +343,23 @@
         [path],
         [arr2, head, sets, sign, level],
         flops=10**8,
+        placed=[arr2],
     )
     arr3 = swap(pay3, TRADES)
-    pay4, g_b_mid = call(gather_kernel, [(32, 48, 128), (1, 512)], [core], [arr3], flops=10**8)
+    pay4, g_b_mid = call(gather_kernel, [(32, 40, 128), (1, 512)], [core], [arr3], flops=10**8, placed=[arr3], final=(1,))
     mine = swap(pay4, "paths")
     other = lax.ppermute(mine, "trades_1", [(0, 1), (1, 0)])
     g_in, g_b_in, g_mid, pay6 = call(
         infer_kernel,
         [(64, 512), (1, 512), (512, 512), (32, 40, 128)],
         [core],
-        [mine, other, w_in, b_in_r, w_mid, b_mid_r, g_b_mid, x_infer, head_shard],
+        [mine, other, w_in, b_in_r, w_mid, b_mid_r, g_b_mid, x_infer_t, head_shard],
         flops=10**9,
+        placed=[mine, other, head_shard],
+        final=(0, 1, 2),
     )
     arr6 = swap(pay6, "paths")
-    g_head_all, exposure = call(finish_kernel, [act, (4, 16)], [], [arr6], flops=10**6)
+    g_head_all, exposure = call(finish_kernel, [act, (4, 16)], [], [arr6], flops=10**6, placed=[arr6], final=(0, 1))
     return (g_in, g_b_in.reshape(-1), g_mid, g_b_mid.reshape(-1), g_head_all, exposure)
 
 

time: 167 us -> 151 us (0.904)
  blocking collectives: 62.8 us -> 91.3 us
  waiting for transfers between devices: 39.5 us -> 17.9 us
  starting transfers between devices: 25.1 us -> 14.9 us
  Pallas kernels: 30.7 us -> 21.6 us
  local copies, waits for them, and re-layouts: 5.23 us -> 1.37 us
    all_to_all x3 -> x4, blocking collectives: 62.8 us -> 91.3 us  [swap(): return lax.all_to_all(x, axis, 0, 0, tiled=True)]
    all_to_all x2 -> x1, waiting for transfers between devices: 38.8 us -> 16.4 us  [swap(): return lax.all_to_all(x, axis, 0, 0, tiled=True)]
    all_to_all x2 -> x1, starting transfers between devices: 21.3 us -> 10.3 us  [swap(): return lax.all_to_all(x, axis, 0, 0, tiled=True)]
    pallas_call x7, Pallas kernels: 30.7 us -> 21.6 us  [call(): pl.pallas_call(kernel, out_shape=shapes, in_specs=[smem] * len(scalars) +...]
    unnamed x12 -> x20, local copies, waits for them, and re-layouts: 5.23 us -> 1.37 us
  transfers between devices with their start and end apart: 3 -> 2, of which waited for: 3 -> 2; matrix products, arithmetic and copies ran while one was open for 1% -> 0% of each run, Pallas kernels for 1% -> 2%
where the time goes in v1:
time: 151 us; the launch traced here: 148 us
  blocking collectives  91.3 us (60%)
  Pallas kernels  21.6 us (14%)
  waiting for transfers between devices  17.9 us (12%)
  starting transfers between devices  14.9 us (10%)
    all_to_all x4, blocking collectives, swap(): return lax.all_to_all(x, axis, 0, 0, tiled=True)  91.3 us
    pallas_call x7, Pallas kernels, call(): pl.pallas_call(kernel, out_shape=shapes, in_specs=[smem] * len(scalars) +...  21.6 us
    all_to_all x1, waiting for transfers between devices, swap(): return lax.all_to_all(x, axis, 0, 0, tiled=True)  16.4 us
    all_to_all x1, starting transfers between devices, swap(): return lax.all_to_all(x, axis, 0, 0, tiled=True)  10.3 us
    ppermute x1, starting transfers between devices, on_device(): other = lax.ppermute(mine, 'trades_1', [(0, 1), (1, 0)])  4.52 us
  transfers between devices with their start and end apart: 2, of which 2 were waited for; matrix products, arithmetic and copies ran while one was open for 0% of the time, Pallas kernels for 2%

profile of v1, /device:TPU:1, one launch (start us, length us, event | category | flops | bytes accessed | tf_op | source)
XLA Modules:
  0.0 147.8 jit_solution(8348692260244724749)
XLA Ops:
  0.6 5.2 %forward_kernel.1 = (f32[16,72,128]{2,1,0:T(8,128)}, f32[512,256]{1,0:T(8,128)S(1)}, f32[512,256]{1,0:T(8,128)}, f32[512,256]{1,0:T(8,128)}, f32[512,256]{1,0:T(...) custom-call(s32[1]{0:T(128)} %bitcast.1.path.own, s32[1]{0:T(128)} %bitcast.2.trade.own, ...), custom_call_target="tpu_custom_call" | custom-call | flops 1000000000 | tf_op jit(solution)/shard_map/forward_kernel/pallas_call | solution.py:286
  5.8 0.0 copy-start
  5.8 10.3 %all-to-all-start = ((f32[16,72,128]{2,1,0:T(8,128)}), f32[16,72,128]{2,1,0:T(8,128)S(1)}, u32[]{:S(2)}, u32[]{:S(2)}) async-start(f32[16,72,128]{2,1,0:T(8,128)} %get-tuple-element.24), calls=%async_computation | async-start | bytes 1179648 | tf_op jit(solution)/shard_map/all_to_all | solution.py:299
  16.2 2.3 %head_grad_kernel.1.g_head = f32[512,256]{1,0:T(8,128)} custom-call(f32[512,256]{1,0:T(8,128)} %get-tuple-element.30.a2_t, f32[256,256]{1,0:T(8,128)} %get-tuple-element.31.dv_t), custom_call_target="tpu_custom_call" | custom-call | flops 400000000 | tf_op jit(solution)/shard_map/head_grad_kernel/pallas_call | solution.py:286
  18.5 16.4 %all-to-all-done.arrived = f32[16,72,128]{2,1,0:T(8,128)S(1)} async-done(((f32[16,72,128]{2,1,0:T(8,128)}), f32[16,72,128]{2,1,0:T(8,128)S(1)}, u32[]{:S(2)}, u32[]{:S(2)}) %all-to-all-start) | async-done | bytes 589856 | tf_op jit(solution)/shard_map/all_to_all | solution.py:299
  34.9 0.0 copy-done
  34.9 5.7 %backward_kernel.1 = f32[32,48,128]{2,1,0:T(8,128)S(1)} custom-call(s32[1]{0:T(128)} %bitcast.2.trade.own, f32[16,72,128]{2,1,0:T(8,128)S(1)} %all-to-all-done.arrived, f32[64,256]{1,0:T(8,128)} %bitcast.25, f32[64,256]{1,0:T(8,128)} %bitcast.26, f32[64,512]{1,0:T(8,128)} %w_in.5, f32[512,64]{1,0:T(8,128)S(1)} %get-tuple-element.25.w_in_t, ...), custom_call_target="tpu_custom_call" | custom-call | flops 1000000000 | tf_op jit(solution)/shard_map/backward_kernel/pallas_call | solution.py:286
  40.6 0.0 copy-start.1
  40.6 0.0 copy-start.4
  40.6 0.0 copy-start.5
  40.6 33.5 %all_to_all.25.arrived = f32[32,48,128]{2,1,0:T(8,128)S(1)} all-to-all(f32[32,48,128]{2,1,0:T(8,128)S(1)} %backward_kernel.1), channel_id=1, replica_groups=mesh['paths'=32,'trades_0'=8,'trades_1'=2] {'paths'}, dimensions={0} | all-to-all | bytes 1572864 | tf_op jit(solution)/shard_map/all_to_all | solution.py:299
  74.1 0.0 copy-start.3
  74.1 0.0 copy-done.1
  74.1 0.0 copy-done.4
  74.1 0.0 copy-done.5
  74.1 0.7 copy-done.3
  74.8 0.7 net_kernel.1
  75.5 12.4 %all_to_all.26.arrived = f32[16,16,128]{2,1,0:T(8,128)S(1)} all-to-all(f32[16,16,128]{2,1,0:T(8,128)S(1)} %get-tuple-element.32), channel_id=1, replica_groups=mesh['paths'=32,'trades_0'=8,'trades_1'=2] {'trades_0','trades_1'}, dimensions={0} | all-to-all | bytes 262144 | tf_op jit(solution)/shard_map/all_to_all | solution.py:299
  87.9 0.7 gather_kernel.1
  88.6 0.0 copy-start.2
  88.6 0.0 copy-start.6
  88.6 0.0 copy-start.8
  88.6 0.0 copy-start.9
  88.7 23.1 %all_to_all.27.mine = f32[32,40,128]{2,1,0:T(8,128)S(1)} all-to-all(f32[32,40,128]{2,1,0:T(8,128)S(1)} %get-tuple-element.33), channel_id=1, replica_groups=mesh['paths'=32,'trades_0'=8,'trades_1'=2] {'paths'}, dimensions={0} | all-to-all | bytes 1310720 | tf_op jit(solution)/shard_map/all_to_all | solution.py:299
  111.8 4.5 %collective-permute-start = (f32[32,40,128]{2,1,0:T(8,128)S(1)}, f32[32,40,128]{2,1,0:T(8,128)S(1)}, u32[]{:S(2)}, u32[]{:S(2)}) collective-permute-start(f32[32,40,128]{2,1,0:T(8,128)S(1)} %all_to_all.27.mine), channel_id=1, source_target_pairs={{0,1},{1,0},{2,3},{3,2},{4,5},{5,4},{6,7},{7,6},{8,9},{9,8},{10,11... | collective-permute-start | bytes 1966088 | tf_op jit(solution)/shard_map/ppermute | solution.py:351
  116.3 1.5 %collective-permute-done.other = f32[32,40,128]{2,1,0:T(8,128)S(1)} collective-permute-done((f32[32,40,128]{2,1,0:T(8,128)S(1)}, f32[32,40,128]{2,1,0:T(8,128)S(1)}, u32[]{:S(2)}, u32[]{:S(2)}) %collective-permute-start) | collective-permute-done | bytes 655392 | tf_op jit(solution)/shard_map/ppermute | solution.py:351
  117.8 0.0 copy-start.7
  117.8 0.0 copy-done.2
  117.8 0.0 copy-done.6
  117.8 0.0 copy-done.8
  117.8 0.0 copy-done.9
  117.8 0.7 copy-done.7
  118.5 6.2 %infer_kernel.1 = (f32[64,512]{1,0:T(8,128)}, f32[1,512]{1,0:T(1,128)}, f32[512,512]{1,0:T(8,128)}, f32[32,40,128]{2,1,0:T(8,128)S(1)}) custom-call(s32[1]{0:T(128)} %bitcast.core.own, f32[32,40,128]{2,1,0:T(8,128)S(1)} %all_to_all.27.mine, f32[32,40,128]{2,1,0:T(8,128)S(1)} %collective-permute-done.other, f32[64,512]{1,0:T(8,128)S(1)} %copy-done.2, ...), custom_call_target="tpu_custom_call" | custom-call | flops 1000000000 | tf_op jit(solution)/shard_map/infer_kernel/pallas_call | solution.py:286
  124.7 22.3 %all_to_all.28.arrived = f32[32,40,128]{2,1,0:T(8,128)S(1)} all-to-all(f32[32,40,128]{2,1,0:T(8,128)S(1)} %get-tuple-element.39), channel_id=1, replica_groups=mesh['paths'=32,'trades_0'=8,'trades_1'=2] {'paths'}, dimensions={0} | all-to-all | bytes 1310720 | tf_op jit(solution)/shard_map/all_to_all | solution.py:299
  146.9 0.8 finish_kernel.1
Async XLA Ops:
  5.8 29.1 %copy-start = (f32[512,512]{1,0:T(8,128)S(1)}, f32[512,512]{1,0:T(8,128)}, u32[]{:S(2)}) copy-start(f32[512,512]{1,0:T(8,128)} %w_mid.5) | copy-start | bytes 3145732
  5.8 29.1 %all-to-all-start = ((f32[16,72,128]{2,1,0:T(8,128)}), f32[16,72,128]{2,1,0:T(8,128)S(1)}, u32[]{:S(2)}, u32[]{:S(2)}) async-start(f32[16,72,128]{2,1,0:T(8,128)} %get-tuple-element.24), calls=%async_computation | async-start | bytes 1179648 | tf_op jit(solution)/shard_map/all_to_all | solution.py:299
  40.6 33.5 %copy-start.1 = (f32[512,256]{1,0:T(8,128)S(1)}, f32[512,256]{1,0:T(8,128)}, u32[]{:S(2)}) copy-start(f32[512,256]{1,0:T(8,128)} %head.3) | copy-start | bytes 1572868
  40.6 33.5 %copy-start.4 = (s32[256]{0:T(256)S(1)}, s32[256]{0:T(256)}, u32[]{:S(2)}) copy-start(s32[256]{0:T(256)} %param.23) | copy-start | bytes 3076
  40.6 33.5 %copy-start.5 = (s32[256]{0:T(256)S(1)}, s32[256]{0:T(256)}, u32[]{:S(2)}) copy-start(s32[256]{0:T(256)} %param.21) | copy-start | bytes 3076
  74.1 0.7 copy-start.3
  88.6 29.2 %copy-start.2 = (f32[64,512]{1,0:T(8,128)S(1)}, f32[64,512]{1,0:T(8,128)}, u32[]{:S(2)}) copy-start(f32[64,512]{1,0:T(8,128)} %w_in.5) | copy-start | bytes 393220
  88.6 29.2 %copy-start.6 = (f32[4,256,64]{1,2,0:T(8,128)S(1)}, f32[4,256,64]{1,2,0:T(8,128)}, u32[]{:S(2)}) copy-start(f32[4,256,64]{1,2,0:T(8,128)} %param.15) | copy-start | bytes 786436
  88.6 29.2 %copy-start.8 = (f32[512]{0:T(512)S(1)}, f32[512]{0:T(512)}, u32[]{:S(2)}) copy-start(f32[512]{0:T(512)} %param.19) | copy-start | bytes 6148
  88.6 29.2 %copy-start.9 = (f32[1,512]{1,0:T(1,128)S(1)}, f32[1,512]{1,0:T(1,128)}, u32[]{:S(2)}) copy-start(f32[1,512]{1,0:T(1,128)} %get-tuple-element.34.g_b_mid) | copy-start | bytes 6148
  111.8 6.0 %collective-permute-start = (f32[32,40,128]{2,1,0:T(8,128)S(1)}, f32[32,40,128]{2,1,0:T(8,128)S(1)}, u32[]{:S(2)}, u32[]{:S(2)}) collective-permute-start(f32[32,40,128]{2,1,0:T(8,128)S(1)} %all_to_all.27.mine), channel_id=1, source_target_pairs={{0,1},{1,0},{2,3},{3,2},{4,5},{5,4},{6,7},{7,6},{8,9},{9,8},{10,11... | collective-permute-start | bytes 1966088 | tf_op jit(solution)/shard_map/ppermute | solution.py:351
  117.8 0.7 copy-start.7

commit v2 on v1

--- a/solution.py
+++ b/solution.py
@@ -9,6 +9,7 @@
 from jax.sharding import PartitionSpec as P
 
 TRADES = ("trades_0", "trades_1")
+PATHS = ("x", "z")
 F32 = jnp.float32
 BF16 = jnp.bfloat16
 
@@ -65,8 +66,8 @@
 
 
 def forward_kernel(
-    path, trade, core, x_t, w_in, b_in, w_mid, b_mid, head, label, sign, level,
-    pay, a1_t, s1_t, s2_t, a2_t, dv_t, w_in_t, w_mid_t,
+    path, trade, core, x_t, w_in, b_in, w_mid, b_mid, head, label, sign, level, sets,
+    pay, a1_t, s1_t, s2_t, a2_t, dv_t, w_in_t, w_mid_t, small,
 ):
     wt = w_in[...].T
     w_in_t[...] = wt
@@ -89,6 +90,10 @@
     pay[:, 0:32, :] = d_a2[:, 0:128].reshape(16, 32, 128)
     pay[:, 32:64, :] = d_a2[:, 128:256].reshape(16, 32, 128)
     w = trade_weights(sign[...], level[...])
+    small[0:1, 0:256] = w
+    small[1:2, 0:256] = sets[...].astype(F32)
+    small[2:3, :] = b_in[...]
+    small[3:4, :] = b_mid[...]
     port = jnp.sum(hd * w, axis=1, keepdims=True)
     for k in range(4):
         col = jnp.broadcast_to(port[128 * k : 128 * k + 128], (128, 128))
@@ -161,10 +166,10 @@
     pay[:, 40:48, :] = g_head[256:512, 128:256].reshape(32, 8, 128)
 
 
-def net_kernel(own, arrived, head, sets, sign, level, pay, head_shard):
+def net_kernel(own, arrived, head, small, pay, head_shard):
     total = jnp.sum(arrived[...], axis=0)
     trunk = total[0:16]
-    w = trade_weights(sign[...], level[...])
+    w = small[0:1, 0:256]
     upper = jnp.concatenate([total[16:24], total[24:32]], axis=1)
     lower = jnp.concatenate([total[32:40], total[40:48]], axis=1)
     g_head = jnp.concatenate([upper, lower], axis=0)
@@ -177,7 +182,7 @@
     second = pl.multiple_of(own[0] * 8 + 256, 8)
     old = jnp.concatenate([head[pl.ds(first, 8), :], head[pl.ds(second, 8), :]], axis=0)
     weighted = halves((old - LEARN * g_head) * w)
-    ids = jnp.broadcast_to(sets[...], (128, 256))
+    ids = jnp.broadcast_to(small[1:2, 0:256].astype(jnp.int32), (128, 256))
     place = lax.broadcasted_iota(jnp.int32, (128, 256), 0) - LANE_NET
     lane = lane_index((16, 128))
     for t in range(16):
@@ -187,7 +192,7 @@
         pay[t] = jnp.where(lane < LANE_NET, trunk, net)
 
 
-def gather_kernel(own, arrived, pay, g_b_mid):
+def gather_kernel(own, arrived, head_shard, pay, g_b_mid):
     total = jnp.sum(arrived[...], axis=0)
     lane = lane_index((16, 128))
     row_lane = lane_index((1, 128))
@@ -215,12 +220,19 @@
     own_rows = jnp.where(eight < LANE_BIN_LATE, own_rows, bias_rows)
     mixed = jnp.where(eight < LANE_NET_UPPER, own_rows, pltpu.roll(upper, net_shift, 1))
     mixed = jnp.where(eight < LANE_NET, mixed, lower)
-    packed = jnp.concatenate(tiles + [mixed], axis=0)
-    pay[...] = jnp.broadcast_to(packed[None], (32, 40, 128))
+    packed = jnp.concatenate(tiles + [mixed, head_shard[...]], axis=0)
+    pay[...] = jnp.broadcast_to(packed[None], (8, 72, 128))
+
+
+def spread_kernel(arrived, trunk, head):
+    lines = arrived[:, 0:40, :].reshape(320, 128)
+    trunk[...] = jnp.broadcast_to(lines[None], (4, 320, 128))
+    heads = arrived[:, 40:72, :].reshape(256, 128)
+    head[...] = jnp.broadcast_to(heads[None], (4, 256, 128))
 
 
 def infer_kernel(
-    own, mine, other, w_in, b_in, w_mid, b_mid, g_b_mid, x_t, head_shard,
+    own, mine, other, w_in, w_mid, small, g_b_mid, x_t,
     g_in_out, g_b_in_out, g_mid_out, pay,
 ):
     first = own[0] == 0
@@ -241,29 +253,31 @@
     g_in_out[...] = g_in
     g_b_in_out[...] = g_b_in
     new_in = halves(w_in[...] - LEARN * g_in)
-    new_b_in = b_in[...] - LEARN * g_b_in
+    new_b_in = small[2:3, :] - LEARN * g_b_in
     new_mid = halves(w_mid[...] - LEARN * g_mid_out[...])
-    new_b_mid = b_mid[...] - LEARN * g_b_mid[...]
+    new_b_mid = small[3:4, :] - LEARN * g_b_mid[...]
     net_head = halves(both)
-    sums = []
+    row = jnp.zeros((1, 128), F32)
+    lane = lane_index((1, 128))
     for d in range(4):
         a1 = softplus(mm(halves(x_t[d].T), new_in) + new_b_in)
         a2 = softplus(mm(halves(a1), new_mid) + new_b_mid)
         netted = mm(halves(a2), net_head)
-        sums.append(jnp.sum(jnp.maximum(netted, 0.0), axis=0, keepdims=True))
-    tile = jnp.concatenate(sums + [jnp.zeros((4, 128), F32)], axis=0)
-    pay[:, 0:32, :] = jnp.broadcast_to(head_shard[...][None], (32, 32, 128))
-    pay[:, 32:40, :] = jnp.broadcast_to(tile[None], (32, 8, 128))
-
-
-def finish_kernel(arrived, g_head, exposure):
+        line = jnp.sum(jnp.maximum(netted, 0.0), axis=0, keepdims=True)
+        moved = pltpu.roll(line, (16 * d - LANE_NET) % 128, 1)
+        row = jnp.where((lane >= 16 * d) & (lane < 16 * d + 16), moved, row)
+    pay[...] = jnp.broadcast_to(row[None], (32, 1, 128))
+
+
+def finish_kernel(arrived, lines, g_head, exposure):
     g_head[0:256, 0:128] = arrived[:, 0:8, :].reshape(256, 128)
     g_head[0:256, 128:256] = arrived[:, 8:16, :].reshape(256, 128)
     g_head[256:512, 0:128] = arrived[:, 16:24, :].reshape(256, 128)
     g_head[256:512, 128:256] = arrived[:, 24:32, :].reshape(256, 128)
-    total = jnp.sum(arrived[:, 32:40, :], axis=0) * (1.0 / 8192.0)
-    moved = pltpu.roll(total, 128 - LANE_NET, 1)
-    exposure[...] = moved[0:4, 0:16]
+    total = jnp.sum(lines[...], axis=0) * (1.0 / 8192.0)
+    for d in range(4):
+        moved = total if d == 0 else pltpu.roll(total, 128 - 16 * d, 1)
+        exposure[d : d + 1, :] = moved[:, 0:16]
 
 
 def keep(a):
@@ -303,7 +317,7 @@
     x_train, value_label, slope_label, x_infer, w_in, b_in, w_mid, b_mid, head,
     trade_set, trade_sign, trade_level,
 ):
-    path = lax.axis_index("paths").astype(jnp.int32).reshape(1)
+    path = lax.axis_index(PATHS).astype(jnp.int32).reshape(1)
     trade = lax.axis_index(TRADES).astype(jnp.int32).reshape(1)
     core = lax.axis_index("trades_1").astype(jnp.int32).reshape(1)
     b_in_r = b_in.reshape(1, -1)
@@ -315,14 +329,14 @@
     x_t = x_train.T
     slope_label_t = slope_label.T
     x_infer_t = x_infer.transpose(0, 2, 1)
-    pay1, a1_t, s1_t, s2_t, a2_t, dv_t, w_in_t, w_mid_t = call(
+    pay1, a1_t, s1_t, s2_t, a2_t, dv_t, w_in_t, w_mid_t, small = call(
         forward_kernel,
-        [(16, 72, 128), act, act, act, act, (256, 256), (512, 64), (512, 512)],
+        [(16, 72, 128), act, act, act, act, (256, 256), (512, 64), (512, 512), (8, 512)],
         [path, trade, core],
-        [x_t, w_in, b_in_r, w_mid, b_mid_r, head, value_label, sign, level],
+        [x_t, w_in, b_in_r, w_mid, b_mid_r, head, value_label, sign, level, sets],
         flops=10**9,
         final=(0, 2, 3, 4, 5),
-        away=[x_t, w_in, w_mid, head, value_label, b_in_r, b_mid_r, sign, level],
+        away=[x_t, w_in, w_mid, head, value_label, b_in_r, b_mid_r, sign, level, sets],
     )
     arr1 = swap(pay1, TRADES)
     (g_head,) = call(head_grad_kernel, [act], [], [a2_t, dv_t], flops=4 * 10**8, final=(0,), away=[a2_t, dv_t])
@@ -336,43 +350,65 @@
         placed=[arr1, w_in_t, w_mid_t, a1_t, w_mid],
         away=[s1_t, s2_t, g_head, x_t, slope_label_t, w_in],
     )
-    arr2 = swap(pay2, "paths")
+    arr2 = swap(pay2, PATHS)
     pay3, head_shard = call(
         net_kernel,
         [(16, 16, 128), (32, 128)],
         [path],
-        [arr2, head, sets, sign, level],
+        [arr2, head, small],
         flops=10**8,
-        placed=[arr2],
+        placed=[arr2, small],
     )
     arr3 = swap(pay3, TRADES)
-    pay4, g_b_mid = call(gather_kernel, [(32, 40, 128), (1, 512)], [core], [arr3], flops=10**8, placed=[arr3], final=(1,))
-    mine = swap(pay4, "paths")
+    pay4, g_b_mid = call(
+        gather_kernel,
+        [(8, 72, 128), (1, 512)],
+        [core],
+        [arr3, head_shard],
+        flops=10**8,
+        placed=[arr3, head_shard],
+        final=(1,),
+    )
+    arr4 = swap(pay4, "z")
+    pay5, pay_head = call(
+        spread_kernel, [(4, 320, 128), (4, 256, 128)], [], [arr4], flops=10**6, placed=[arr4]
+    )
+    mine = swap(pay5, "x").reshape(32, 40, 128)
+    pay_head, mine = lax.optimization_barrier((pay_head, mine))
+    arr_head = swap(pay_head, "x").reshape(32, 32, 128)
     other = lax.ppermute(mine, "trades_1", [(0, 1), (1, 0)])
     g_in, g_b_in, g_mid, pay6 = call(
         infer_kernel,
-        [(64, 512), (1, 512), (512, 512), (32, 40, 128)],
+        [(64, 512), (1, 512), (512, 512), (32, 1, 128)],
         [core],
-        [mine, other, w_in, b_in_r, w_mid, b_mid_r, g_b_mid, x_infer_t, head_shard],
+        [mine, other, w_in, w_mid, small, g_b_mid, x_infer_t],
         flops=10**9,
-        placed=[mine, other, head_shard],
+        placed=[mine, other, small],
         final=(0, 1, 2),
     )
-    arr6 = swap(pay6, "paths")
-    g_head_all, exposure = call(finish_kernel, [act, (4, 16)], [], [arr6], flops=10**6, placed=[arr6], final=(0, 1))
+    arr6 = swap(pay6, PATHS)
+    g_head_all, exposure = call(
+        finish_kernel,
+        [act, (4, 16)],
+        [],
+        [arr_head, arr6],
+        flops=10**6,
+        placed=[arr_head, arr6],
+        final=(0, 1),
+    )
     return (g_in, g_b_in.reshape(-1), g_mid, g_b_mid.reshape(-1), g_head_all, exposure)
 
 
 def solution(mesh):
-    torus = Mesh(mesh.devices.reshape(mesh.shape["paths"], 8, 2), ("paths", "trades_0", "trades_1"))
+    torus = Mesh(mesh.devices.reshape(4, 8, 8, 2), PATHS + TRADES)
     return jax.shard_map(
         on_device,
         mesh=torus,
         in_specs=(
-            P("paths", None),
-            P("paths", TRADES),
-            P("paths", None),
-            P(None, "paths", None),
+            P(PATHS, None),
+            P(PATHS, TRADES),
+            P(PATHS, None),
+            P(None, PATHS, None),
             P(),
             P(),
             P(),

time: 151 us -> 148 us (0.980); the launches traced: 148 us -> 147 us
  blocking collectives: 91.3 us -> 86.4 us
  starting transfers between devices: 14.9 us -> 17.9 us
    all_to_all x4 -> x5, blocking collectives: 91.3 us -> 86.4 us  [swap(): return lax.all_to_all(x, axis, 0, 0, tiled=True)]
    all_to_all x1 -> x2, starting transfers between devices: 10.3 us -> 14 us  [swap(): return lax.all_to_all(x, axis, 0, 0, tiled=True)]
    all_to_all x1 -> x2, waiting for transfers between devices: 16.4 us -> 18.8 us  [swap(): return lax.all_to_all(x, axis, 0, 0, tiled=True)]
    ppermute x1, waiting for transfers between devices: 1.52 us -> 0.01 us  [on_device(): other = lax.ppermute(mine, 'trades_1', [(0, 1), (1, 0)])]
    pallas_call x7 -> x8, Pallas kernels: 21.6 us -> 22.6 us  [call(): pl.pallas_call(kernel, out_shape=shapes, in_specs=[smem] * len(scalars) +...]
  transfers between devices with their start and end apart: 2 -> 3, of which waited for: 2 -> 2; matrix products, arithmetic and copies ran while one was open for 0% -> 0% of each run, Pallas kernels for 2% -> 6%
where the time goes in v2:
time: 148 us; the launch traced here: 147 us
  blocking collectives  86.4 us (58%)
  Pallas kernels  22.6 us (15%)
  waiting for transfers between devices  18.8 us (13%)
  starting transfers between devices  17.9 us (12%)
    all_to_all x5, blocking collectives, swap(): return lax.all_to_all(x, axis, 0, 0, tiled=True)  86.4 us
    pallas_call x8, Pallas kernels, call(): pl.pallas_call(kernel, out_shape=shapes, in_specs=[smem] * len(scalars) +...  22.6 us
    all_to_all x2, waiting for transfers between devices, swap(): return lax.all_to_all(x, axis, 0, 0, tiled=True)  18.8 us
    all_to_all x2, starting transfers between devices, swap(): return lax.all_to_all(x, axis, 0, 0, tiled=True)  14 us
    ppermute x1, starting transfers between devices, on_device(): other = lax.ppermute(mine, 'trades_1', [(0, 1), (1, 0)])  3.86 us
  transfers between devices with their start and end apart: 3, of which 2 were waited for; matrix products, arithmetic and copies ran while one was open for 0% of the time, Pallas kernels for 6%

profile of v2, /device:TPU:1, one launch (start us, length us, event | category | flops | bytes accessed | tf_op | source)
XLA Modules:
  0.0 147.0 jit_solution(658076050422160719)
XLA Ops:
  0.6 5.2 %forward_kernel.1 = (f32[16,72,128]{2,1,0:T(8,128)}, f32[512,256]{1,0:T(8,128)S(1)}, f32[512,256]{1,0:T(8,128)}, f32[512,256]{1,0:T(8,128)}, f32[512,256]{1,0:T(...) custom-call(s32[1]{0:T(128)} %bitcast.1.path.own, ...), custom_call_target="tpu_custom_call" | custom-call | flops 1000000000 | tf_op jit(solution)/shard_map/forward_kernel/pallas_call | solution.py:300
  5.9 0.0 copy-start
  5.9 10.4 %all-to-all-start = ((f32[16,72,128]{2,1,0:T(8,128)}), f32[16,72,128]{2,1,0:T(8,128)S(1)}, u32[]{:S(2)}, u32[]{:S(2)}) async-start(f32[16,72,128]{2,1,0:T(8,128)} %get-tuple-element.29), calls=%async_computation | async-start | bytes 1179648 | tf_op jit(solution)/shard_map/all_to_all | solution.py:313
  16.2 2.4 %head_grad_kernel.1.g_head = f32[512,256]{1,0:T(8,128)} custom-call(f32[512,256]{1,0:T(8,128)} %get-tuple-element.35.a2_t, f32[256,256]{1,0:T(8,128)} %get-tuple-element.36.dv_t), custom_call_target="tpu_custom_call" | custom-call | flops 400000000 | tf_op jit(solution)/shard_map/head_grad_kernel/pallas_call | solution.py:300
  18.6 16.4 %all-to-all-done.arrived = f32[16,72,128]{2,1,0:T(8,128)S(1)} async-done(((f32[16,72,128]{2,1,0:T(8,128)}), f32[16,72,128]{2,1,0:T(8,128)S(1)}, u32[]{:S(2)}, u32[]{:S(2)}) %all-to-all-start) | async-done | bytes 589856 | tf_op jit(solution)/shard_map/all_to_all | solution.py:313
  34.9 0.0 copy-done
  34.9 5.7 %backward_kernel.1 = f32[32,48,128]{2,1,0:T(8,128)S(1)} custom-call(s32[1]{0:T(128)} %bitcast.2.trade.own, f32[16,72,128]{2,1,0:T(8,128)S(1)} %all-to-all-done.arrived, f32[64,256]{1,0:T(8,128)} %bitcast.21, f32[64,256]{1,0:T(8,128)} %bitcast.22, f32[64,512]{1,0:T(8,128)} %w_in.5, f32[512,64]{1,0:T(8,128)S(1)} %get-tuple-element.30.w_in_t, ...), custom_call_target="tpu_custom_call" | custom-call | flops 1000000000 | tf_op jit(solution)/shard_map/backward_kernel/pallas_call | solution.py:300
  40.6 0.0 copy-start.1
  40.6 33.5 %all_to_all.35.arrived = f32[32,48,128]{2,1,0:T(8,128)S(1)} all-to-all(f32[32,48,128]{2,1,0:T(8,128)S(1)} %backward_kernel.1), channel_id=1, replica_groups=mesh['x'=4,'z'=8,'trades_0'=8,'trades_1'=2] {'x','z'}, dimensions={0} | all-to-all | bytes 1572864 | tf_op jit(solution)/shard_map/all_to_all | solution.py:313
  74.1 0.0 copy-done.1
  74.1 0.7 net_kernel.1
  74.8 12.4 %all_to_all.36.arrived = f32[16,16,128]{2,1,0:T(8,128)S(1)} all-to-all(f32[16,16,128]{2,1,0:T(8,128)S(1)} %get-tuple-element.38), channel_id=1, replica_groups=mesh['x'=4,'z'=8,'trades_0'=8,'trades_1'=2] {'trades_0','trades_1'}, dimensions={0} | all-to-all | bytes 262144 | tf_op jit(solution)/shard_map/all_to_all | solution.py:313
  87.3 0.7 gather_kernel.1
  88.0 16.4 %all_to_all.37.arrived = f32[8,72,128]{2,1,0:T(8,128)S(1)} all-to-all(f32[8,72,128]{2,1,0:T(8,128)S(1)} %get-tuple-element.40), channel_id=1, replica_groups=mesh['x'=4,'z'=8,'trades_0'=8,'trades_1'=2] {'z'}, dimensions={0} | all-to-all | bytes 589824 | tf_op jit(solution)/shard_map/all_to_all | solution.py:313
  104.4 0.9 spread_kernel.1
  105.3 12.4 %all_to_all.38 = f32[4,320,128]{2,1,0:T(8,128)S(1)} all-to-all(f32[4,320,128]{2,1,0:T(8,128)S(1)} %get-tuple-element.42), channel_id=1, replica_groups=mesh['x'=4,'z'=8,'trades_0'=8,'trades_1'=2] {'x'}, dimensions={0} | all-to-all | bytes 1310720 | tf_op jit(solution)/shard_map/all_to_all | solution.py:313
  117.7 0.0 copy-start.2
  117.7 0.0 copy-start.3
  117.7 3.9 %collective-permute-start = (f32[32,40,128]{2,1,0:T(8,128)S(1)}, f32[32,40,128]{2,1,0:T(8,128)S(1)}, u32[]{:S(2)}, u32[]{:S(2)}) collective-permute-start(f32[32,40,128]{2,1,0:T(8,128)S(1)} %bitcast.16), channel_id=1, source_target_pairs={{0,1},{1,0},{2,3},{3,2},{4,5},{5,4},{6,7},{7,6},{8,9},{9,8},{10,11... | collective-permute-start | bytes 1966088 | tf_op jit(solution)/shard_map/ppermute | solution.py:379
  121.6 3.7 %all-to-all-start.5 = ((f32[4,256,128]{2,1,0:T(8,128)}), f32[4,256,128]{2,1,0:T(8,128)S(1)}, u32[]{:S(2)}, u32[]{:S(2)}) async-start(f32[4,256,128]{2,1,0:T(8,128)} %get-tuple-element.48), calls=%async_computation.5 | async-start | bytes 1048576 | tf_op jit(solution)/shard_map/all_to_all | solution.py:313
  125.2 0.0 copy-start.4
  125.2 0.0 collective-permute-done.other
  125.3 0.0 copy-done.2
  125.3 0.0 copy-done.3
  125.3 0.6 copy-done.4
  125.9 6.2 %infer_kernel.1 = (f32[64,512]{1,0:T(8,128)}, f32[1,512]{1,0:T(1,128)}, f32[512,512]{1,0:T(8,128)}, f32[32,1,128]{2,1,0:T(1,128)S(1)}) custom-call(s32[1]{0:T(128)} %bitcast.core.own, f32[32,40,128]{2,1,0:T(8,128)S(1)} %bitcast.17, f32[32,40,128]{2,1,0:T(8,128)S(1)} %collective-permute-done.other, f32[64,512]{1,0:T(8,128)S(1)} %copy-done.2, ...), custom_call_target="tpu_custom_call" | custom-call | flops 1000000000 | tf_op jit(solution)/shard_map/infer_kernel/pallas_call | solution.py:300
  132.1 2.4 %all-to-all-done.5 = f32[4,256,128]{2,1,0:T(8,128)S(1)} async-done(((f32[4,256,128]{2,1,0:T(8,128)}), f32[4,256,128]{2,1,0:T(8,128)S(1)}, u32[]{:S(2)}, u32[]{:S(2)}) %all-to-all-start.5) | async-done | bytes 524320 | tf_op jit(solution)/shard_map/all_to_all | solution.py:313
  134.6 11.6 %all_to_all.39.lines = f32[32,1,128]{2,1,0:T(1,128)S(1)} all-to-all(f32[32,1,128]{2,1,0:T(1,128)S(1)} %get-tuple-element.49), channel_id=1, replica_groups=mesh['x'=4,'z'=8,'trades_0'=8,'trades_1'=2] {'x','z'}, dimensions={0} | all-to-all | bytes 32768 | tf_op jit(solution)/shard_map/all_to_all | solution.py:313
  146.2 0.8 finish_kernel.1
Async XLA Ops:
  5.9 29.1 %copy-start = (f32[512,512]{1,0:T(8,128)S(1)}, f32[512,512]{1,0:T(8,128)}, u32[]{:S(2)}) copy-start(f32[512,512]{1,0:T(8,128)} %w_mid.5) | copy-start | bytes 3145732
  5.9 29.1 %all-to-all-start = ((f32[16,72,128]{2,1,0:T(8,128)}), f32[16,72,128]{2,1,0:T(8,128)S(1)}, u32[]{:S(2)}, u32[]{:S(2)}) async-start(f32[16,72,128]{2,1,0:T(8,128)} %get-tuple-element.29), calls=%async_computation | async-start | bytes 1179648 | tf_op jit(solution)/shard_map/all_to_all | solution.py:313
  40.6 33.5 %copy-start.1 = (f32[512,256]{1,0:T(8,128)S(1)}, f32[512,256]{1,0:T(8,128)}, u32[]{:S(2)}) copy-start(f32[512,256]{1,0:T(8,128)} %head.3) | copy-start | bytes 1572868
  117.7 7.6 %copy-start.2 = (f32[64,512]{1,0:T(8,128)S(1)}, f32[64,512]{1,0:T(8,128)}, u32[]{:S(2)}) copy-start(f32[64,512]{1,0:T(8,128)} %w_in.5) | copy-start | bytes 393220
  117.7 7.6 %copy-start.3 = (f32[4,256,64]{1,2,0:T(8,128)S(1)}, f32[4,256,64]{1,2,0:T(8,128)}, u32[]{:S(2)}) copy-start(f32[4,256,64]{1,2,0:T(8,128)} %param.15) | copy-start | bytes 786436
  117.7 7.6 %collective-permute-start = (f32[32,40,128]{2,1,0:T(8,128)S(1)}, f32[32,40,128]{2,1,0:T(8,128)S(1)}, u32[]{:S(2)}, u32[]{:S(2)}) collective-permute-start(f32[32,40,128]{2,1,0:T(8,128)S(1)} %bitcast.16), channel_id=1, source_target_pairs={{0,1},{1,0},{2,3},{3,2},{4,5},{5,4},{6,7},{7,6},{8,9},{9,8},{10,11... | collective-permute-start | bytes 1966088 | tf_op jit(solution)/shard_map/ppermute | solution.py:379
  121.6 13.0 %all-to-all-start.5 = ((f32[4,256,128]{2,1,0:T(8,128)}), f32[4,256,128]{2,1,0:T(8,128)S(1)}, u32[]{:S(2)}, u32[]{:S(2)}) async-start(f32[4,256,128]{2,1,0:T(8,128)} %get-tuple-element.48), calls=%async_computation.5 | async-start | bytes 1048576 | tf_op jit(solution)/shard_map/all_to_all | solution.py:313
  125.2 0.7 copy-start.4

commit v3 on v2

--- a/solution.py
+++ b/solution.py
@@ -42,15 +42,8 @@
     return dot(left[0], right[0]) + (dot(left[0], right[1]) + dot(left[1], right[0]))
 
 
-def softplus_sigmoid(z):
-    e = jnp.exp(-jnp.abs(z))
-    act = jnp.maximum(z, 0.0) + jnp.log1p(e)
-    slope = jnp.where(z >= 0, 1.0, e) / (1.0 + e)
-    return act, slope
-
-
 def softplus(z):
-    return jnp.maximum(z, 0.0) + jnp.log1p(jnp.exp(-jnp.abs(z)))
+    return jnp.maximum(z, 0.0) + jnp.log(1.0 + jnp.exp(-jnp.abs(z)))
 
 
 def trade_weights(sign, level):
@@ -67,39 +60,51 @@
 
 def forward_kernel(
     path, trade, core, x_t, w_in, b_in, w_mid, b_mid, head, label, sign, level, sets,
-    pay, a1_t, s1_t, s2_t, a2_t, dv_t, w_in_t, w_mid_t, small,
+    own, other, a1_t, a2_t, dv_t, w_mid_t, small,
 ):
+    first = core[0] == 0
     wt = w_in[...].T
-    w_in_t[...] = wt
     z1 = mm(halves(wt), halves(x_t[...])) + column_of(b_in[...])
-    a1, s1 = softplus_sigmoid(z1)
+    a1 = softplus(z1)
     a1_t[...] = a1
-    s1_t[...] = s1
     mt = w_mid[...].T
     w_mid_t[...] = mt
     z2 = mm(halves(mt), halves(a1)) + column_of(b_mid[...])
-    a2, s2 = softplus_sigmoid(z2)
+    a2 = softplus(z2)
     a2_t[...] = a2
-    s2_t[...] = s2
     hd = head[...]
-    hp = halves(hd)
     values = mm(halves(hd.T), halves(a2))
     err = (values - label[...].T) * VALUE_SCALE
     dv_t[...] = err
-    d_a2 = mm(hp, halves(err))
-    pay[:, 0:32, :] = d_a2[:, 0:128].reshape(16, 32, 128)
-    pay[:, 32:64, :] = d_a2[:, 128:256].reshape(16, 32, 128)
+    err_p = halves(err)
+    d_a2 = mm(halves(hd), err_p)
     w = trade_weights(sign[...], level[...])
+
+    def place(block, rows, start):
+        pairs = block.reshape(8, 2, rows, 128)
+        even = pairs[:, 0]
+        odd = pairs[:, 1]
+        own[:, start : start + rows, :] = jnp.where(first, even, odd)
+        other[:, start : start + rows, :] = jnp.where(first, odd, even)
+
+    place(d_a2[:, 0:128], 32, 0)
+    place(d_a2[:, 128:256], 32, 32)
     small[0:1, 0:256] = w
     small[1:2, 0:256] = sets[...].astype(F32)
     small[2:3, :] = b_in[...]
     small[3:4, :] = b_mid[...]
     port = jnp.sum(hd * w, axis=1, keepdims=True)
+    rows = []
     for k in range(4):
         col = jnp.broadcast_to(port[128 * k : 128 * k + 128], (128, 128))
-        row = col.T[0:1]
-        pay[:, 64 + k : 65 + k, :] = jnp.broadcast_to(row[None], (16, 1, 128))
-    pay[:, 68:72, :] = jnp.zeros((16, 4, 128), F32)
+        rows.append(col.T[0:1])
+    tile = jnp.concatenate(rows + [jnp.zeros((4, 128), F32)], axis=0)
+    own[:, 64:72, :] = jnp.broadcast_to(tile[None], (8, 8, 128))
+    other[:, 64:72, :] = jnp.broadcast_to(tile[None], (8, 8, 128))
+
+
+def join_kernel(own, got, out):
+    out[...] = own[...] + got[...]
 
 
 def head_grad_kernel(a2_t, dv_t, out):
@@ -107,8 +112,8 @@
 
 
 def backward_kernel(
-    own, arrived, x_t, slope_label_t, w_in, w_in_t, w_mid, w_mid_t, a1_t, s1_t, s2_t, g_head,
-    pay, u2_s, q_s, z_s,
+    own, arrived, x_t, slope_label_t, w_in, w_mid, w_mid_t, a1_t, a2_t, g_head,
+    pay, s2_s, u2_s, q_s, z_s,
 ):
     rows = pl.ds(pl.multiple_of(own[0] * 32, 32), 32)
     total = jnp.sum(arrived[...], axis=0)
@@ -116,15 +121,19 @@
     port = jnp.concatenate(
         [column_of(total[64 + k : 65 + k]) for k in range(4)], axis=0
     ) * PORT_SCALE
-    s1 = s1_t[...]
-    s2 = s2_t[...]
+    a1 = a1_t[...]
+    a2 = a2_t[...]
+    s1 = 1.0 - jnp.exp(-a1)
+    s2 = 1.0 - jnp.exp(-a2)
+    s2_s[...] = s2
     u2 = port * s2
     u2_s[...] = u2
-    v1 = mm(halves(w_mid[...]), halves(u2))
+    mid_p = halves(w_mid[...])
+    v1 = mm(mid_p, halves(u2))
     u1 = v1 * s1
     slopes = mm(halves(w_in[...]), halves(u1))
     d_slope = (slopes - slope_label_t[...]) * SLOPE_SCALE
-    du1 = mm(halves(w_in_t[...]), halves(d_slope))
+    du1 = mm(halves(w_in[...].T), halves(d_slope))
     dv1 = du1 * s1
     ds1 = du1 * v1
     dv1_p = halves(dv1)
@@ -132,10 +141,10 @@
     du2_s2 = du2 * s2
     g_port = jnp.sum(du2_s2, axis=1, keepdims=True)
     q_s[...] = du2_s2 * port * (1.0 - s2)
-    dz2 = d_a2 * s2_t[rows, :] + q_s[rows, :]
+    dz2 = d_a2 * s2_s[rows, :] + q_s[rows, :]
     z_s[...] = jnp.zeros_like(z_s)
     z_s[rows, :] = dz2
-    da1 = mm(halves(w_mid[...]), halves(z_s[...]))
+    da1 = mm(mid_p, halves(z_s[...]))
     dz1 = da1 * s1 + (ds1 * s1 * (1.0 - s1)) * (1.0 / 16.0)
     g_b_in = jnp.sum(dz1, axis=1, keepdims=True)
     none = jnp.zeros((64, 256), F32)
@@ -144,7 +153,7 @@
     mid_b = jnp.concatenate([none, u2_s[rows, :], few], axis=0)
     slope_rows = jnp.concatenate([d_slope * (1.0 / 16.0), none], axis=0)
     x_rows = jnp.concatenate([x_t[...], none], axis=0)
-    ext = mm(halves(a1_t[...]), halves(mid_a), NT)
+    ext = mm(halves(a1), halves(mid_a), NT)
     ext = ext + mm(dv1_p, halves(mid_b), NT)
     ext = ext + mm(halves(u1), halves(slope_rows), NT)
     ext = ext + mm(halves(dz1), halves(x_rows), NT)
@@ -253,6 +262,7 @@
     g_in_out[...] = g_in
     g_b_in_out[...] = g_b_in
     new_in = halves(w_in[...] - LEARN * g_in)
+    deep_in = jnp.concatenate([new_in[0], new_in[0], new_in[1]], axis=0)
     new_b_in = small[2:3, :] - LEARN * g_b_in
     new_mid = halves(w_mid[...] - LEARN * g_mid_out[...])
     new_b_mid = small[3:4, :] - LEARN * g_b_mid[...]
@@ -260,7 +270,10 @@
     row = jnp.zeros((1, 128), F32)
     lane = lane_index((1, 128))
     for d in range(4):
-        a1 = softplus(mm(halves(x_t[d].T), new_in) + new_b_in)
+        high, low = halves(x_t[d].T)
+        rows = jnp.concatenate([high, low, high], axis=1)
+        first_pre = jnp.dot(rows, deep_in, preferred_element_type=F32)
+        a1 = softplus(first_pre + new_b_in)
         a2 = softplus(mm(halves(a1), new_mid) + new_b_mid)
         netted = mm(halves(a2), net_head)
         line = jnp.sum(jnp.maximum(netted, 0.0), axis=0, keepdims=True)
@@ -329,26 +342,38 @@
     x_t = x_train.T
     slope_label_t = slope_label.T
     x_infer_t = x_infer.transpose(0, 2, 1)
-    pay1, a1_t, s1_t, s2_t, a2_t, dv_t, w_in_t, w_mid_t, small = call(
+    own, other, a1_t, a2_t, dv_t, w_mid_t, small = call(
         forward_kernel,
-        [(16, 72, 128), act, act, act, act, (256, 256), (512, 64), (512, 512), (8, 512)],
+        [(8, 72, 128), (8, 72, 128), act, act, (256, 256), (512, 512), (8, 512)],
         [path, trade, core],
         [x_t, w_in, b_in_r, w_mid, b_mid_r, head, value_label, sign, level, sets],
         flops=10**9,
-        final=(0, 2, 3, 4, 5),
+        final=(4,),
         away=[x_t, w_in, w_mid, head, value_label, b_in_r, b_mid_r, sign, level, sets],
     )
-    arr1 = swap(pay1, TRADES)
-    (g_head,) = call(head_grad_kernel, [act], [], [a2_t, dv_t], flops=4 * 10**8, final=(0,), away=[a2_t, dv_t])
+    got = lax.ppermute(other, "trades_1", [(0, 1), (1, 0)])
+    (g_head,) = call(
+        head_grad_kernel,
+        [act],
+        [],
+        [a2_t, dv_t],
+        flops=4 * 10**8,
+        placed=[a2_t],
+        away=[dv_t],
+        final=(0,),
+    )
+    (pay1,) = call(join_kernel, [(8, 72, 128)], [], [own, got], flops=10**6, placed=[own, got])
+    pay1, g_head = lax.optimization_barrier((pay1, g_head))
+    arr1 = swap(pay1, "trades_0")
     (pay2,) = call(
         backward_kernel,
         [(32, 48, 128)],
         [trade],
-        [arr1, x_t, slope_label_t, w_in, w_in_t, w_mid, w_mid_t, a1_t, s1_t, s2_t, g_head],
-        scratch=[act, act, act],
+        [arr1, x_t, slope_label_t, w_in, w_mid, w_mid_t, a1_t, a2_t, g_head],
+        scratch=[act, act, act, act],
         flops=10**9,
-        placed=[arr1, w_in_t, w_mid_t, a1_t, w_mid],
-        away=[s1_t, s2_t, g_head, x_t, slope_label_t, w_in],
+        placed=[arr1, w_mid_t, a1_t, a2_t],
+        away=[x_t, slope_label_t, w_in, g_head],
     )
     arr2 = swap(pay2, PATHS)
     pay3, head_shard = call(

time: 148 us -> 145 us (0.980)
  blocking collectives: 86.4 us -> 103 us
  waiting for transfers between devices: 18.8 us -> 3.76 us
  Pallas kernels: 22.6 us -> 20.4 us
  starting transfers between devices: 17.9 us -> 15.7 us
    all_to_all x5 -> x6, blocking collectives: 86.4 us -> 103 us  [swap(): return lax.all_to_all(x, axis, 0, 0, tiled=True)]
    all_to_all x2 -> x1, waiting for transfers between devices: 18.8 us -> 3.76 us  [swap(): return lax.all_to_all(x, axis, 0, 0, tiled=True)]
    all_to_all x2 -> x1, starting transfers between devices: 14 us -> 3.48 us  [swap(): return lax.all_to_all(x, axis, 0, 0, tiled=True)]
    ppermute x0 -> x1, starting transfers between devices: none -> 8.73 us  [on_device(): got = lax.ppermute(other, 'trades_1', [(0, 1), (1, 0)])]
    pallas_call x8 -> x9, Pallas kernels: 22.6 us -> 20.4 us  [call(): pl.pallas_call(kernel, out_shape=shapes, in_specs=[smem] * len(scalars) +...]
  transfers between devices with their start and end apart: 3 -> 3, of which waited for: 2 -> 1; matrix products, arithmetic and copies ran while one was open for 0% -> 0% of each run, Pallas kernels for 6% -> 5%
where the time goes in v3:
time: 145 us
  blocking collectives  103 us (71%)
  Pallas kernels  20.4 us (14%)
  starting transfers between devices  15.7 us (11%)
  waiting for transfers between devices  3.76 us (3%)
    all_to_all x6, blocking collectives, swap(): return lax.all_to_all(x, axis, 0, 0, tiled=True)  103 us
    pallas_call x9, Pallas kernels, call(): pl.pallas_call(kernel, out_shape=shapes, in_specs=[smem] * len(scalars) +...  20.4 us
    ppermute x1, starting transfers between devices, on_device(): got = lax.ppermute(other, 'trades_1', [(0, 1), (1, 0)])  8.73 us
    all_to_all x1, waiting for transfers between devices, swap(): return lax.all_to_all(x, axis, 0, 0, tiled=True)  3.76 us
    all_to_all x1, starting transfers between devices, swap(): return lax.all_to_all(x, axis, 0, 0, tiled=True)  3.48 us
    ppermute x1, starting transfers between devices, on_device(): other = lax.ppermute(mine, 'trades_1', [(0, 1), (1, 0)])  3.45 us
  transfers between devices with their start and end apart: 3, of which 1 were waited for; matrix products, arithmetic and copies ran while one was open for 0% of the time, Pallas kernels for 5%

profile of v3, /device:TPU:1, one launch (start us, length us, event | category | flops | bytes accessed | tf_op | source)
XLA Modules:
  0.0 144.5 jit_solution(9089639397893515585)
XLA Ops:
  0.6 4.6 %forward_kernel.1 = (f32[8,72,128]{2,1,0:T(8,128)S(1)}, f32[8,72,128]{2,1,0:T(8,128)S(1)}, f32[512,256]{1,0:T(8,128)S(1)}, f32[512,256]{1,0:T(8,128)S(1)}, f32[2...) custom-call(s32[1]{0:T(128)} %bitcast.1.path.own, s32[1]{0:T(128)} %bitcast.2.trade.own, ...), custom_call_target="tpu_custom_call" | custom-call | flops 1000000000 | tf_op jit(solution)/shard_map/forward_kernel/pallas_call | solution.py:313
  5.2 8.7 %collective-permute-start = (f32[8,72,128]{2,1,0:T(8,128)S(1)}, f32[8,72,128]{2,1,0:T(8,128)S(1)}, u32[]{:S(2)}, u32[]{:S(2)}) collective-permute-start(f32[8,72,128]{2,1,0:T(8,128)S(1)} %get-tuple-element.30), channel_id=1, source_target_pairs={{0,1},{1,0},{2,3},{3,2},{4,5},{5,4},{6,7},{7,6},{8,9},{9,8},{10,11... | collective-permute-start | bytes 884744 | tf_op jit(solution)/shard_map/ppermute | solution.py:354
  14.0 2.2 %head_grad_kernel.1.g_head = f32[512,256]{1,0:T(8,128)} custom-call(f32[512,256]{1,0:T(8,128)S(1)} %get-tuple-element.31.a2_t, f32[256,256]{1,0:T(8,128)} %get-tuple-element.32.dv_t), custom_call_target="tpu_custom_call" | custom-call | flops 400000000 | tf_op jit(solution)/shard_map/head_grad_kernel/pallas_call | solution.py:313
  16.1 0.0 copy-start
  16.1 0.0 collective-permute-done.got
  16.2 15.2 %all_to_all.35.arrived = f32[8,72,128]{2,1,0:T(8,128)S(1)} all-to-all(f32[8,72,128]{2,1,0:T(8,128)S(1)} %join_kernel.1), channel_id=1, replica_groups=mesh['x'=4,'z'=8,'trades_0'=8,'trades_1'=2] {'trades_0'}, dimensions={0} | all-to-all | bytes 589824 | tf_op jit(solution)/shard_map/all_to_all | solution.py:326
  31.4 0.0 copy-done
  31.4 5.4 %backward_kernel.1 = f32[32,48,128]{2,1,0:T(8,128)S(1)} custom-call(s32[1]{0:T(128)} %bitcast.2.trade.own, f32[8,72,128]{2,1,0:T(8,128)S(1)} %all_to_all.35.arrived, f32[64,256]{1,0:T(8,128)} %bitcast.21, f32[64,256]{1,0:T(8,128)} %bitcast.22, f32[64,512]{1,0:T(8,128)} %w_in.5, f32[512,512]{1,0:T(8,128)S(1)} %copy-done, ...), custom_call_target="tpu_custom_call" | custom-call | flops 1000000000 | tf_op jit(solution)/shard_map/backward_kernel/pallas_call | solution.py:313
  36.8 0.0 copy-start.1
  36.8 31.2 %all_to_all.36.arrived = f32[32,48,128]{2,1,0:T(8,128)S(1)} all-to-all(f32[32,48,128]{2,1,0:T(8,128)S(1)} %backward_kernel.1), channel_id=1, replica_groups=mesh['x'=4,'z'=8,'trades_0'=8,'trades_1'=2] {'x','z'}, dimensions={0} | all-to-all | bytes 1572864 | tf_op jit(solution)/shard_map/all_to_all | solution.py:326
  68.0 0.0 copy-done.1
  68.0 0.7 net_kernel.1
  68.8 16.3 %all_to_all.37.arrived = f32[16,16,128]{2,1,0:T(8,128)S(1)} all-to-all(f32[16,16,128]{2,1,0:T(8,128)S(1)} %get-tuple-element.38), channel_id=1, replica_groups=mesh['x'=4,'z'=8,'trades_0'=8,'trades_1'=2] {'trades_0','trades_1'}, dimensions={0} | all-to-all | bytes 262144 | tf_op jit(solution)/shard_map/all_to_all | solution.py:326
  85.1 0.7 gather_kernel.1
  85.8 16.1 %all_to_all.38.arrived = f32[8,72,128]{2,1,0:T(8,128)S(1)} all-to-all(f32[8,72,128]{2,1,0:T(8,128)S(1)} %get-tuple-element.40), channel_id=1, replica_groups=mesh['x'=4,'z'=8,'trades_0'=8,'trades_1'=2] {'z'}, dimensions={0} | all-to-all | bytes 589824 | tf_op jit(solution)/shard_map/all_to_all | solution.py:326
  101.9 0.9 spread_kernel.1
  102.8 12.8 %all_to_all.39 = f32[4,320,128]{2,1,0:T(8,128)S(1)} all-to-all(f32[4,320,128]{2,1,0:T(8,128)S(1)} %get-tuple-element.42), channel_id=1, replica_groups=mesh['x'=4,'z'=8,'trades_0'=8,'trades_1'=2] {'x'}, dimensions={0} | all-to-all | bytes 1310720 | tf_op jit(solution)/shard_map/all_to_all | solution.py:326
  115.6 0.0 copy-start.2
  115.6 0.0 copy-start.3
  115.6 3.5 %collective-permute-start.1 = (f32[32,40,128]{2,1,0:T(8,128)S(1)}, f32[32,40,128]{2,1,0:T(8,128)S(1)}, u32[]{:S(2)}, u32[]{:S(2)}) collective-permute-start(f32[32,40,128]{2,1,0:T(8,128)S(1)} %bitcast.16), channel_id=1, source_target_pairs={{0,1},{1,0},{2,3},{3,2},{4,5},{5,4},{6,7},{7,6},{8,9},{9,8},{10,11... | collective-permute-start | bytes 1966088 | tf_op jit(solution)/shard_map/ppermute | solution.py:404
  119.0 3.5 %all-to-all-start.5 = ((f32[4,256,128]{2,1,0:T(8,128)}), f32[4,256,128]{2,1,0:T(8,128)S(1)}, u32[]{:S(2)}, u32[]{:S(2)}) async-start(f32[4,256,128]{2,1,0:T(8,128)} %get-tuple-element.48), calls=%async_computation.5 | async-start | bytes 1048576 | tf_op jit(solution)/shard_map/all_to_all | solution.py:326
  122.5 0.0 copy-start.4
  122.5 0.0 collective-permute-done.1.other
  122.5 0.0 copy-done.2
  122.6 0.0 copy-done.3
  122.6 0.6 copy-done.4
  123.2 5.1 %infer_kernel.1 = (f32[64,512]{1,0:T(8,128)}, f32[1,512]{1,0:T(1,128)}, f32[512,512]{1,0:T(8,128)}, f32[32,1,128]{2,1,0:T(1,128)S(1)}) custom-call(s32[1]{0:T(128)} %bitcast.core.own, f32[32,40,128]{2,1,0:T(8,128)S(1)} %bitcast.17, f32[32,40,128]{2,1,0:T(8,128)S(1)} %collective-permute-done.1.other, f32[64,512]{1,0:T(8,128)S(1)} %copy-done.2, ...), custom_call_target="tpu_custom_call" | custom-call | flops 1000000000 | tf_op jit(solution)/shard_map/infer_kernel/pallas_call | solution.py:313
  128.3 3.8 %all-to-all-done.5 = f32[4,256,128]{2,1,0:T(8,128)S(1)} async-done(((f32[4,256,128]{2,1,0:T(8,128)}), f32[4,256,128]{2,1,0:T(8,128)S(1)}, u32[]{:S(2)}, u32[]{:S(2)}) %all-to-all-start.5) | async-done | bytes 524320 | tf_op jit(solution)/shard_map/all_to_all | solution.py:326
  132.0 11.6 %all_to_all.40.lines = f32[32,1,128]{2,1,0:T(1,128)S(1)} all-to-all(f32[32,1,128]{2,1,0:T(1,128)S(1)} %get-tuple-element.49), channel_id=1, replica_groups=mesh['x'=4,'z'=8,'trades_0'=8,'trades_1'=2] {'x','z'}, dimensions={0} | all-to-all | bytes 32768 | tf_op jit(solution)/shard_map/all_to_all | solution.py:326
  143.7 0.8 finish_kernel.1
  (1 shorter events, 0.0 us)
Async XLA Ops:
  5.2 10.9 %collective-permute-start = (f32[8,72,128]{2,1,0:T(8,128)S(1)}, f32[8,72,128]{2,1,0:T(8,128)S(1)}, u32[]{:S(2)}, u32[]{:S(2)}) collective-permute-start(f32[8,72,128]{2,1,0:T(8,128)S(1)} %get-tuple-element.30), channel_id=1, source_target_pairs={{0,1},{1,0},{2,3},{3,2},{4,5},{5,4},{6,7},{7,6},{8,9},{9,8},{10,11... | collective-permute-start | bytes 884744 | tf_op jit(solution)/shard_map/ppermute | solution.py:354
  16.1 15.3 %copy-start = (f32[512,512]{1,0:T(8,128)S(1)}, f32[512,512]{1,0:T(8,128)}, u32[]{:S(2)}) copy-start(f32[512,512]{1,0:T(8,128)} %w_mid.5) | copy-start | bytes 3145732
  36.8 31.3 %copy-start.1 = (f32[512,256]{1,0:T(8,128)S(1)}, f32[512,256]{1,0:T(8,128)}, u32[]{:S(2)}) copy-start(f32[512,256]{1,0:T(8,128)} %head.3) | copy-start | bytes 1572868
  115.6 7.0 %copy-start.2 = (f32[64,512]{1,0:T(8,128)S(1)}, f32[64,512]{1,0:T(8,128)}, u32[]{:S(2)}) copy-start(f32[64,512]{1,0:T(8,128)} %w_in.5) | copy-start | bytes 393220
  115.6 7.0 %copy-start.3 = (f32[4,256,64]{1,2,0:T(8,128)S(1)}, f32[4,256,64]{1,2,0:T(8,128)}, u32[]{:S(2)}) copy-start(f32[4,256,64]{1,2,0:T(8,128)} %param.15) | copy-start | bytes 786436
  115.6 7.0 %collective-permute-start.1 = (f32[32,40,128]{2,1,0:T(8,128)S(1)}, f32[32,40,128]{2,1,0:T(8,128)S(1)}, u32[]{:S(2)}, u32[]{:S(2)}) collective-permute-start(f32[32,40,128]{2,1,0:T(8,128)S(1)} %bitcast.16), channel_id=1, source_target_pairs={{0,1},{1,0},{2,3},{3,2},{4,5},{5,4},{6,7},{7,6},{8,9},{9,8},{10,11... | collective-permute-start | bytes 1966088 | tf_op jit(solution)/shard_map/ppermute | solution.py:404
  119.0 13.0 %all-to-all-start.5 = ((f32[4,256,128]{2,1,0:T(8,128)}), f32[4,256,128]{2,1,0:T(8,128)S(1)}, u32[]{:S(2)}, u32[]{:S(2)}) async-start(f32[4,256,128]{2,1,0:T(8,128)} %get-tuple-element.48), calls=%async_computation.5 | async-start | bytes 1048576 | tf_op jit(solution)/shard_map/all_to_all | solution.py:326
  122.5 0.7 copy-start.4

commit v4 on v3

--- a/solution.py
+++ b/solution.py
@@ -42,6 +42,13 @@
     return dot(left[0], right[0]) + (dot(left[0], right[1]) + dot(left[1], right[0]))
 
 
+def mm_narrow(left, right, dims=NN):
+    both = jnp.concatenate(right, axis=1 if dims is NN else 0)
+    wide = lax.dot_general(left[0], both, dims, preferred_element_type=F32)
+    rest = lax.dot_general(left[1], right[0], dims, preferred_element_type=F32)
+    return wide[:, 0:128] + (wide[:, 128:256] + rest)
+
+
 def softplus(z):
     return jnp.maximum(z, 0.0) + jnp.log(1.0 + jnp.exp(-jnp.abs(z)))
 
@@ -60,7 +67,7 @@
 
 def forward_kernel(
     path, trade, core, x_t, w_in, b_in, w_mid, b_mid, head, label, sign, level, sets,
-    own, other, a1_t, a2_t, dv_t, w_mid_t, small,
+    own, other, a1_t, a2_t, dv_t, small,
 ):
     first = core[0] == 0
     wt = w_in[...].T
@@ -68,7 +75,6 @@
     a1 = softplus(z1)
     a1_t[...] = a1
     mt = w_mid[...].T
-    w_mid_t[...] = mt
     z2 = mm(halves(mt), halves(a1)) + column_of(b_mid[...])
     a2 = softplus(z2)
     a2_t[...] = a2
@@ -112,7 +118,7 @@
 
 
 def backward_kernel(
-    own, arrived, x_t, slope_label_t, w_in, w_mid, w_mid_t, a1_t, a2_t, g_head,
+    own, arrived, x_t, slope_label_t, w_in, w_mid, a1_t, a2_t, g_head,
     pay, s2_s, u2_s, q_s, z_s,
 ):
     rows = pl.ds(pl.multiple_of(own[0] * 32, 32), 32)
@@ -137,7 +143,7 @@
     dv1 = du1 * s1
     ds1 = du1 * v1
     dv1_p = halves(dv1)
-    du2 = mm(halves(w_mid_t[...]), dv1_p)
+    du2 = mm(halves(w_mid[...].T), dv1_p)
     du2_s2 = du2 * s2
     g_port = jnp.sum(du2_s2, axis=1, keepdims=True)
     q_s[...] = du2_s2 * port * (1.0 - s2)
@@ -153,10 +159,10 @@
     mid_b = jnp.concatenate([none, u2_s[rows, :], few], axis=0)
     slope_rows = jnp.concatenate([d_slope * (1.0 / 16.0), none], axis=0)
     x_rows = jnp.concatenate([x_t[...], none], axis=0)
-    ext = mm(halves(a1), halves(mid_a), NT)
-    ext = ext + mm(dv1_p, halves(mid_b), NT)
-    ext = ext + mm(halves(u1), halves(slope_rows), NT)
-    ext = ext + mm(halves(dz1), halves(x_rows), NT)
+    ext = mm_narrow(halves(a1), halves(mid_a), NT)
+    ext = ext + mm_narrow(dv1_p, halves(mid_b), NT)
+    ext = ext + mm_narrow(halves(u1), halves(slope_rows), NT)
+    ext = ext + mm_narrow(halves(dz1), halves(x_rows), NT)
     lane = lane_index((512, 128))
     ext = jnp.where(lane == LANE_BIN, g_b_in, ext)
     ext = jnp.where(lane == LANE_PORT, g_port, ext)
@@ -201,7 +207,7 @@
         pay[t] = jnp.where(lane < LANE_NET, trunk, net)
 
 
-def gather_kernel(own, arrived, head_shard, pay, g_b_mid):
+def gather_kernel(own, arrived, head_shard, pay, g_b_mid, g_b_near):
     total = jnp.sum(arrived[...], axis=0)
     lane = lane_index((16, 128))
     row_lane = lane_index((1, 128))
@@ -220,6 +226,7 @@
                 line = part[0:8] if shift == 0 else pltpu.roll(part[0:8], shift, 1)
                 bias = jnp.where((row_lane >= to) & (row_lane < to + 8), line[r : r + 1], bias)
         g_b_mid[:, 128 * k : 128 * k + 128] = bias
+        g_b_near[:, 128 * k : 128 * k + 128] = bias
         tiles.append(jnp.where(first, block[0:8], block[8:16]))
     upper, lower = total[0:8], total[8:16]
     own_rows = jnp.where(first, upper, lower)
@@ -233,11 +240,16 @@
     pay[...] = jnp.broadcast_to(packed[None], (8, 72, 128))
 
 
-def spread_kernel(arrived, trunk, head):
-    lines = arrived[:, 0:40, :].reshape(320, 128)
-    trunk[...] = jnp.broadcast_to(lines[None], (4, 320, 128))
-    heads = arrived[:, 40:72, :].reshape(256, 128)
-    head[...] = jnp.broadcast_to(heads[None], (4, 256, 128))
+def spread_kernel(arrived, out):
+    lines = arrived[...].reshape(576, 128)
+    out[...] = jnp.broadcast_to(lines[None], (4, 576, 128))
+
+
+def head_out_kernel(arrived, g_head):
+    g_head[0:256, 0:128] = arrived[:, 40:48, :].reshape(256, 128)
+    g_head[0:256, 128:256] = arrived[:, 48:56, :].reshape(256, 128)
+    g_head[256:512, 0:128] = arrived[:, 56:64, :].reshape(256, 128)
+    g_head[256:512, 128:256] = arrived[:, 64:72, :].reshape(256, 128)
 
 
 def infer_kernel(
@@ -275,18 +287,14 @@
         first_pre = jnp.dot(rows, deep_in, preferred_element_type=F32)
         a1 = softplus(first_pre + new_b_in)
         a2 = softplus(mm(halves(a1), new_mid) + new_b_mid)
-        netted = mm(halves(a2), net_head)
+        netted = mm_narrow(halves(a2), net_head)
         line = jnp.sum(jnp.maximum(netted, 0.0), axis=0, keepdims=True)
         moved = pltpu.roll(line, (16 * d - LANE_NET) % 128, 1)
         row = jnp.where((lane >= 16 * d) & (lane < 16 * d + 16), moved, row)
     pay[...] = jnp.broadcast_to(row[None], (32, 1, 128))
 
 
-def finish_kernel(arrived, lines, g_head, exposure):
-    g_head[0:256, 0:128] = arrived[:, 0:8, :].reshape(256, 128)
-    g_head[0:256, 128:256] = arrived[:, 8:16, :].reshape(256, 128)
-    g_head[256:512, 0:128] = arrived[:, 16:24, :].reshape(256, 128)
-    g_head[256:512, 128:256] = arrived[:, 24:32, :].reshape(256, 128)
+def finish_kernel(lines, exposure):
     total = jnp.sum(lines[...], axis=0) * (1.0 / 8192.0)
     for d in range(4):
         moved = total if d == 0 else pltpu.roll(total, 128 - 16 * d, 1)
@@ -342,13 +350,12 @@
     x_t = x_train.T
     slope_label_t = slope_label.T
     x_infer_t = x_infer.transpose(0, 2, 1)
-    own, other, a1_t, a2_t, dv_t, w_mid_t, small = call(
+    own, other, a1_t, a2_t, dv_t, small = call(
         forward_kernel,
-        [(8, 72, 128), (8, 72, 128), act, act, (256, 256), (512, 512), (8, 512)],
+        [(8, 72, 128), (8, 72, 128), act, act, (256, 256), (8, 512)],
         [path, trade, core],
         [x_t, w_in, b_in_r, w_mid, b_mid_r, head, value_label, sign, level, sets],
         flops=10**9,
-        final=(4,),
         away=[x_t, w_in, w_mid, head, value_label, b_in_r, b_mid_r, sign, level, sets],
     )
     got = lax.ppermute(other, "trades_1", [(0, 1), (1, 0)])
@@ -358,9 +365,7 @@
         [],
         [a2_t, dv_t],
         flops=4 * 10**8,
-        placed=[a2_t],
-        away=[dv_t],
-        final=(0,),
+        placed=[a2_t, dv_t],
     )
     (pay1,) = call(join_kernel, [(8, 72, 128)], [], [own, got], flops=10**6, placed=[own, got])
     pay1, g_head = lax.optimization_barrier((pay1, g_head))
@@ -369,11 +374,10 @@
         backward_kernel,
         [(32, 48, 128)],
         [trade],
-        [arr1, x_t, slope_label_t, w_in, w_mid, w_mid_t, a1_t, a2_t, g_head],
+        [arr1, x_t, slope_label_t, w_in, w_mid, a1_t, a2_t, g_head],
         scratch=[act, act, act, act],
         flops=10**9,
-        placed=[arr1, w_mid_t, a1_t, a2_t],
-        away=[x_t, slope_label_t, w_in, g_head],
+        placed=[arr1, w_mid, a1_t, a2_t, g_head, x_t, slope_label_t, w_in],
     )
     arr2 = swap(pay2, PATHS)
     pay3, head_shard = call(
@@ -385,9 +389,9 @@
         placed=[arr2, small],
     )
     arr3 = swap(pay3, TRADES)
-    pay4, g_b_mid = call(
+    pay4, g_b_mid, g_b_near = call(
         gather_kernel,
-        [(8, 72, 128), (1, 512)],
+        [(8, 72, 128), (1, 512), (1, 512)],
         [core],
         [arr3, head_shard],
         flops=10**8,
@@ -395,31 +399,25 @@
         final=(1,),
     )
     arr4 = swap(pay4, "z")
-    pay5, pay_head = call(
-        spread_kernel, [(4, 320, 128), (4, 256, 128)], [], [arr4], flops=10**6, placed=[arr4]
-    )
-    mine = swap(pay5, "x").reshape(32, 40, 128)
-    pay_head, mine = lax.optimization_barrier((pay_head, mine))
-    arr_head = swap(pay_head, "x").reshape(32, 32, 128)
+    (pay5,) = call(spread_kernel, [(4, 576, 128)], [], [arr4], flops=10**6, placed=[arr4])
+    mine = swap(pay5, "x").reshape(32, 72, 128)
     other = lax.ppermute(mine, "trades_1", [(0, 1), (1, 0)])
+    (g_head_all,) = call(
+        head_out_kernel, [act], [], [mine], flops=10**8, placed=[mine], final=(0,)
+    )
+    other, g_head_all = lax.optimization_barrier((other, g_head_all))
     g_in, g_b_in, g_mid, pay6 = call(
         infer_kernel,
         [(64, 512), (1, 512), (512, 512), (32, 1, 128)],
         [core],
-        [mine, other, w_in, w_mid, small, g_b_mid, x_infer_t],
+        [mine, other, w_in, w_mid, small, g_b_near, x_infer_t],
         flops=10**9,
-        placed=[mine, other, small],
+        placed=[mine, other, small, g_b_near],
         final=(0, 1, 2),
     )
     arr6 = swap(pay6, PATHS)
-    g_head_all, exposure = call(
-        finish_kernel,
-        [act, (4, 16)],
-        [],
-        [arr_head, arr6],
-        flops=10**6,
-        placed=[arr_head, arr6],
-        final=(0, 1),
+    (exposure,) = call(
+        finish_kernel, [(4, 16)], [], [arr6], flops=10**6, placed=[arr6], final=(0,)
     )
     return (g_in, g_b_in.reshape(-1), g_mid, g_b_mid.reshape(-1), g_head_all, exposure)
 

time: 145 us -> 140 us (0.966)
  blocking collectives: 103 us -> 108 us
  Pallas kernels: 20.4 us -> 16.4 us
  starting transfers between devices: 15.7 us -> 12.2 us
    all_to_all x6, blocking collectives: 103 us -> 108 us  [swap(): return lax.all_to_all(x, axis, 0, 0, tiled=True)]
    pallas_call x9 -> x10, Pallas kernels: 20.4 us -> 16.4 us  [call(): pl.pallas_call(kernel, out_shape=shapes, in_specs=[smem] * len(scalars) +...]
    all_to_all x1 -> x0, waiting for transfers between devices: 3.76 us -> none  [swap(): return lax.all_to_all(x, axis, 0, 0, tiled=True)]
    all_to_all x1 -> x0, starting transfers between devices: 3.48 us -> none  [swap(): return lax.all_to_all(x, axis, 0, 0, tiled=True)]
    ppermute x1, waiting for transfers between devices: 0.01 us -> 1.62 us  [on_device(): other = lax.ppermute(mine, 'trades_1', [(0, 1), (1, 0)])]
  transfers between devices with their start and end apart: 3 -> 2, of which waited for: 1 -> 2; matrix products, arithmetic and copies ran while one was open for 0% -> 0% of each run, Pallas kernels for 5% -> 1%
where the time goes in v4:
time: 140 us
  blocking collectives  108 us (77%)
  Pallas kernels  16.4 us (12%)
  starting transfers between devices  12.2 us (9%)
  waiting for transfers between devices  2.34 us (2%)
    all_to_all x6, blocking collectives, swap(): return lax.all_to_all(x, axis, 0, 0, tiled=True)  108 us
    pallas_call x10, Pallas kernels, call(): pl.pallas_call(kernel, out_shape=shapes, in_specs=[smem] * len(scalars) +...  16.4 us
    ppermute x1, starting transfers between devices, on_device(): got = lax.ppermute(other, 'trades_1', [(0, 1), (1, 0)])  8.75 us
    ppermute x1, starting transfers between devices, on_device(): other = lax.ppermute(mine, 'trades_1', [(0, 1), (1, 0)])  3.43 us
  transfers between devices with their start and end apart: 2, of which 2 were waited for; matrix products, arithmetic and copies ran while one was open for 0% of the time, Pallas kernels for 1%

profile of v4, /device:TPU:1, one launch (start us, length us, event | category | flops | bytes accessed | tf_op | source)
XLA Modules:
  0.0 140.1 jit_solution(7343230493978836635)
XLA Ops:
  0.6 4.1 %forward_kernel.1 = (f32[8,72,128]{2,1,0:T(8,128)S(1)}, f32[8,72,128]{2,1,0:T(8,128)S(1)}, f32[512,256]{1,0:T(8,128)S(1)}, f32[512,256]{1,0:T(8,128)S(1)}, f32[256,256]{1,0:T(8,128)S(1)}, /*index=5*/f32[8,512]{1,0:T(8,128)S(1)}) custom-call(s32[1]{0:T(128)} %bitcast.1.path.own, s32[1]{0:T(128)} %bitcast.2.trade.own, s32[1]{0:T(128)} %bitcast.core.own, ...), custom_call_target="tpu_custom_call" | custom-call | flops 1000000000 | tf_op jit(solution)/shard_map/forward_kernel/pallas_call | solution.py:321
  4.7 8.7 %collective-permute-start = (f32[8,72,128]{2,1,0:T(8,128)S(1)}, f32[8,72,128]{2,1,0:T(8,128)S(1)}, u32[]{:S(2)}, u32[]{:S(2)}) collective-permute-start(f32[8,72,128]{2,1,0:T(8,128)S(1)} %get-tuple-element.26), channel_id=1, source_target_pairs={{0,1},{1,0},{2,3},{3,2},{4,5},{5,4},{6,7},{7,6},{8,9},{9,8},{10,11... | collective-permute-start | bytes 884744 | tf_op jit(solution)/shard_map/ppermute | solution.py:361
  13.5 0.0 copy-start
  13.5 0.0 copy-start.2
  13.5 0.0 copy-start.4
  13.5 0.0 copy-start.5
  13.5 0.4 head_grad_kernel.1.g_head
  13.9 0.7 collective-permute-done.got
  14.7 15.0 %all_to_all.30.arrived = f32[8,72,128]{2,1,0:T(8,128)S(1)} all-to-all(f32[8,72,128]{2,1,0:T(8,128)S(1)} %join_kernel.1), channel_id=1, replica_groups=mesh['x'=4,'z'=8,'trades_0'=8,'trades_1'=2] {'trades_0'}, dimensions={0} | all-to-all | bytes 589824 | tf_op jit(solution)/shard_map/all_to_all | solution.py:334
  29.7 0.0 copy-done
  29.7 0.0 copy-done.2
  29.7 0.0 copy-done.4
  29.7 0.0 copy-done.5
  29.7 4.3 %backward_kernel.1 = f32[32,48,128]{2,1,0:T(8,128)S(1)} custom-call(s32[1]{0:T(128)} %bitcast.2.trade.own, f32[8,72,128]{2,1,0:T(8,128)S(1)} %all_to_all.30.arrived, f32[64,256]{1,0:T(8,128)S(1)} %bitcast.19, f32[64,256]{1,0:T(8,128)S(1)} %bitcast.20, f32[64,512]{1,0:T(8,128)S(1)} %copy-done.2, f32[512,512]{1,0:T(8,128)S(1)} %copy-done, ...), custom_call_target="tpu_custom_call" | custom-call | flops 1000000000 | tf_op jit(solution)/shard_map/backward_kernel/pallas_call | solution.py:321
  34.0 0.0 copy-start.1
  34.1 31.1 %all_to_all.31.arrived = f32[32,48,128]{2,1,0:T(8,128)S(1)} all-to-all(f32[32,48,128]{2,1,0:T(8,128)S(1)} %backward_kernel.1), channel_id=1, replica_groups=mesh['x'=4,'z'=8,'trades_0'=8,'trades_1'=2] {'x','z'}, dimensions={0} | all-to-all | bytes 1572864 | tf_op jit(solution)/shard_map/all_to_all | solution.py:334
  65.2 0.0 copy-done.1
  65.2 0.7 net_kernel.1
  65.9 16.0 %all_to_all.32.arrived = f32[16,16,128]{2,1,0:T(8,128)S(1)} all-to-all(f32[16,16,128]{2,1,0:T(8,128)S(1)} %get-tuple-element.33), channel_id=1, replica_groups=mesh['x'=4,'z'=8,'trades_0'=8,'trades_1'=2] {'trades_0','trades_1'}, dimensions={0} | all-to-all | bytes 262144 | tf_op jit(solution)/shard_map/all_to_all | solution.py:334
  81.9 0.7 gather_kernel.1
  82.6 16.1 %all_to_all.33.arrived = f32[8,72,128]{2,1,0:T(8,128)S(1)} all-to-all(f32[8,72,128]{2,1,0:T(8,128)S(1)} %get-tuple-element.35), channel_id=1, replica_groups=mesh['x'=4,'z'=8,'trades_0'=8,'trades_1'=2] {'z'}, dimensions={0} | all-to-all | bytes 589824 | tf_op jit(solution)/shard_map/all_to_all | solution.py:334
  98.7 0.1 spread_kernel.1
  98.8 18.5 %all_to_all.34 = f32[4,576,128]{2,1,0:T(8,128)S(1)} all-to-all(f32[4,576,128]{2,1,0:T(8,128)S(1)} %spread_kernel.1), channel_id=1, replica_groups=mesh['x'=4,'z'=8,'trades_0'=8,'trades_1'=2] {'x'}, dimensions={0} | all-to-all | bytes 2359296 | tf_op jit(solution)/shard_map/all_to_all | solution.py:334
  117.3 0.0 copy-start.3
  117.3 3.4 %collective-permute-start.1 = (f32[32,72,128]{2,1,0:T(8,128)S(1)}, f32[32,72,128]{2,1,0:T(8,128)S(1)}, u32[]{:S(2)}, u32[]{:S(2)}) collective-permute-start(f32[32,72,128]{2,1,0:T(8,128)S(1)} %bitcast.14), channel_id=1, source_target_pairs={{0,1},{1,0},{2,3},{3,2},{4,5},{5,4},{6,7},{7,6},{8,9},{9,8},{10,11... | collective-permute-start | bytes 3538952 | tf_op jit(solution)/shard_map/ppermute | solution.py:404
  120.7 0.8 head_out_kernel.1
  121.6 1.6 %collective-permute-done.1.other = f32[32,72,128]{2,1,0:T(8,128)S(1)} collective-permute-done((f32[32,72,128]{2,1,0:T(8,128)S(1)}, f32[32,72,128]{2,1,0:T(8,128)S(1)}, u32[]{:S(2)}, u32[]{:S(2)}) %collective-permute-start.1) | collective-permute-done | bytes 1179680 | tf_op jit(solution)/shard_map/ppermute | solution.py:404
  123.2 0.0 copy-done.3
  123.2 4.6 %infer_kernel.1 = (f32[64,512]{1,0:T(8,128)}, f32[1,512]{1,0:T(1,128)}, f32[512,512]{1,0:T(8,128)}, f32[32,1,128]{2,1,0:T(1,128)S(1)}) custom-call(s32[1]{0:T(128)} %bitcast.core.own, f32[32,72,128]{2,1,0:T(8,128)S(1)} %bitcast.16, f32[32,72,128]{2,1,0:T(8,128)S(1)} %collective-permute-done.1.other, f32[64,512]{1,0:T(8,128)S(1)} %copy-done.2, ...), custom_call_target="tpu_custom_call" | custom-call | flops 1000000000 | tf_op jit(solution)/shard_map/infer_kernel/pallas_call | solution.py:321
  127.8 11.6 %all_to_all.35.lines = f32[32,1,128]{2,1,0:T(1,128)S(1)} all-to-all(f32[32,1,128]{2,1,0:T(1,128)S(1)} %get-tuple-element.43), channel_id=1, replica_groups=mesh['x'=4,'z'=8,'trades_0'=8,'trades_1'=2] {'x','z'}, dimensions={0} | all-to-all | bytes 32768 | tf_op jit(solution)/shard_map/all_to_all | solution.py:334
  139.4 0.7 finish_kernel.1
  (1 shorter events, 0.0 us)
Async XLA Ops:
  4.7 9.9 %collective-permute-start = (f32[8,72,128]{2,1,0:T(8,128)S(1)}, f32[8,72,128]{2,1,0:T(8,128)S(1)}, u32[]{:S(2)}, u32[]{:S(2)}) collective-permute-start(f32[8,72,128]{2,1,0:T(8,128)S(1)} %get-tuple-element.26), channel_id=1, source_target_pairs={{0,1},{1,0},{2,3},{3,2},{4,5},{5,4},{6,7},{7,6},{8,9},{9,8},{10,11... | collective-permute-start | bytes 884744 | tf_op jit(solution)/shard_map/ppermute | solution.py:361
  13.5 16.2 %copy-start = (f32[512,512]{1,0:T(8,128)S(1)}, f32[512,512]{1,0:T(8,128)}, u32[]{:S(2)}) copy-start(f32[512,512]{1,0:T(8,128)} %w_mid.5) | copy-start | bytes 3145732
  13.5 16.2 %copy-start.2 = (f32[64,512]{1,0:T(8,128)S(1)}, f32[64,512]{1,0:T(8,128)}, u32[]{:S(2)}) copy-start(f32[64,512]{1,0:T(8,128)} %w_in.5) | copy-start | bytes 393220
  13.5 16.2 %copy-start.4 = (f32[256,64]{0,1:T(8,128)S(1)}, f32[256,64]{0,1:T(8,128)}, u32[]{:S(2)}) copy-start(f32[256,64]{0,1:T(8,128)} %param.12) | copy-start | bytes 196612
  13.5 16.2 %copy-start.5 = (f32[256,64]{0,1:T(8,128)S(1)}, f32[256,64]{0,1:T(8,128)}, u32[]{:S(2)}) copy-start(f32[256,64]{0,1:T(8,128)} %param.14) | copy-start | bytes 196612
  34.0 31.2 %copy-start.1 = (f32[512,256]{1,0:T(8,128)S(1)}, f32[512,256]{1,0:T(8,128)}, u32[]{:S(2)}) copy-start(f32[512,256]{1,0:T(8,128)} %head.3) | copy-start | bytes 1572868
  117.3 5.9 %copy-start.3 = (f32[4,256,64]{1,2,0:T(8,128)S(1)}, f32[4,256,64]{1,2,0:T(8,128)}, u32[]{:S(2)}) copy-start(f32[4,256,64]{1,2,0:T(8,128)} %param.15) | copy-start | bytes 786436
  117.3 5.9 %collective-permute-start.1 = (f32[32,72,128]{2,1,0:T(8,128)S(1)}, f32[32,72,128]{2,1,0:T(8,128)S(1)}, u32[]{:S(2)}, u32[]{:S(2)}) collective-permute-start(f32[32,72,128]{2,1,0:T(8,128)S(1)} %bitcast.14), channel_id=1, source_target_pairs={{0,1},{1,0},{2,3},{3,2},{4,5},{5,4},{6,7},{7,6},{8,9},{9,8},{10,11... | collective-permute-start | bytes 3538952 | tf_op jit(solution)/shard_map/ppermute | solution.py:404

commit v5 on v4

--- a/solution.py
+++ b/solution.py
@@ -245,6 +245,10 @@
     out[...] = jnp.broadcast_to(lines[None], (4, 576, 128))
 
 
+def trim_kernel(arrived, out):
+    out[...] = arrived[:, 0:40, :]
+
+
 def head_out_kernel(arrived, g_head):
     g_head[0:256, 0:128] = arrived[:, 40:48, :].reshape(256, 128)
     g_head[0:256, 128:256] = arrived[:, 48:56, :].reshape(256, 128)
@@ -254,14 +258,14 @@
 
 def infer_kernel(
     own, mine, other, w_in, w_mid, small, g_b_mid, x_t,
-    g_in_out, g_b_in_out, g_mid_out, pay,
+    g_in_out, g_b_in_out, g_mid_out, pay, g_in_s, g_b_in_s, g_mid_s, sems,
 ):
     first = own[0] == 0
     for k in range(4):
         a = mine[:, 8 * k : 8 * k + 8, :].reshape(256, 128)
         b = other[:, 8 * k : 8 * k + 8, :].reshape(256, 128)
-        g_mid_out[0:256, 128 * k : 128 * k + 128] = jnp.where(first, a, b)
-        g_mid_out[256:512, 128 * k : 128 * k + 128] = jnp.where(first, b, a)
+        g_mid_s[0:256, 128 * k : 128 * k + 128] = jnp.where(first, a, b)
+        g_mid_s[256:512, 128 * k : 128 * k + 128] = jnp.where(first, b, a)
     near = mine[:, 32:40, :].reshape(256, 128)
     away = other[:, 32:40, :].reshape(256, 128)
     upper = jnp.where(first, near, away)
@@ -271,12 +275,19 @@
     g_b_in = flat[LANE_BIN_LATE : LANE_BIN_LATE + 1]
     net_shift = (LANE_NET - LANE_NET_UPPER) % 128
     both = jnp.concatenate([pltpu.roll(near, net_shift, 1), near], axis=0)
-    g_in_out[...] = g_in
-    g_b_in_out[...] = g_b_in
+    g_in_s[...] = g_in
+    g_b_in_s[...] = g_b_in
+    copies = [
+        pltpu.make_async_copy(g_mid_s, g_mid_out, sems.at[0]),
+        pltpu.make_async_copy(g_in_s, g_in_out, sems.at[1]),
+        pltpu.make_async_copy(g_b_in_s, g_b_in_out, sems.at[2]),
+    ]
+    for copy in copies:
+        copy.start()
     new_in = halves(w_in[...] - LEARN * g_in)
     deep_in = jnp.concatenate([new_in[0], new_in[0], new_in[1]], axis=0)
     new_b_in = small[2:3, :] - LEARN * g_b_in
-    new_mid = halves(w_mid[...] - LEARN * g_mid_out[...])
+    new_mid = halves(w_mid[...] - LEARN * g_mid_s[...])
     new_b_mid = small[3:4, :] - LEARN * g_b_mid[...]
     net_head = halves(both)
     row = jnp.zeros((1, 128), F32)
@@ -292,6 +303,8 @@
         moved = pltpu.roll(line, (16 * d - LANE_NET) % 128, 1)
         row = jnp.where((lane >= 16 * d) & (lane < 16 * d + 16), moved, row)
     pay[...] = jnp.broadcast_to(row[None], (32, 1, 128))
+    for copy in copies:
+        copy.wait()
 
 
 def finish_kernel(lines, exposure):
@@ -309,11 +322,12 @@
     return pltpu.with_memory_space_constraint(a, pltpu.HBM)
 
 
-def call(kernel, outs, scalars, args, scratch=(), flops=0, placed=(), final=(), away=()):
+def call(kernel, outs, scalars, args, scratch=(), flops=0, placed=(), final=(), away=(), copies=0):
     shapes = tuple(
         pltpu.HBM(s, F32) if i in final else pltpu.VMEM(s, F32)
         for i, s in enumerate(outs)
     )
+    semaphores = [pltpu.SemaphoreType.DMA((copies,))] if copies else []
     vmem = pl.BlockSpec(memory_space=pltpu.VMEM)
     smem = pl.BlockSpec(memory_space=pltpu.SMEM)
     args = [keep(a) if any(a is p for p in placed) else a for a in args]
@@ -322,8 +336,10 @@
         kernel,
         out_shape=shapes,
         in_specs=[smem] * len(scalars) + [vmem] * len(args),
-        out_specs=tuple(vmem for _ in outs),
-        scratch_shapes=[pltpu.VMEM(s, F32) for s in scratch],
+        out_specs=tuple(
+            pl.BlockSpec(memory_space=pl.ANY) if i < copies else vmem for i in range(len(outs))
+        ),
+        scratch_shapes=[pltpu.VMEM(s, F32) for s in scratch] + semaphores,
         cost_estimate=pl.CostEstimate(flops=flops, transcendentals=0, bytes_accessed=0),
         compiler_params=pltpu.CompilerParams(vmem_limit_bytes=24 * 2**20),
         name=kernel.__name__,
@@ -401,7 +417,8 @@
     arr4 = swap(pay4, "z")
     (pay5,) = call(spread_kernel, [(4, 576, 128)], [], [arr4], flops=10**6, placed=[arr4])
     mine = swap(pay5, "x").reshape(32, 72, 128)
-    other = lax.ppermute(mine, "trades_1", [(0, 1), (1, 0)])
+    (trunk,) = call(trim_kernel, [(32, 40, 128)], [], [mine], flops=10**6, placed=[mine])
+    other = lax.ppermute(trunk, "trades_1", [(0, 1), (1, 0)])
     (g_head_all,) = call(
         head_out_kernel, [act], [], [mine], flops=10**8, placed=[mine], final=(0,)
     )
@@ -410,9 +427,11 @@
         infer_kernel,
         [(64, 512), (1, 512), (512, 512), (32, 1, 128)],
         [core],
-        [mine, other, w_in, w_mid, small, g_b_near, x_infer_t],
+        [trunk, other, w_in, w_mid, small, g_b_near, x_infer_t],
         flops=10**9,
-        placed=[mine, other, small, g_b_near],
+        placed=[trunk, other, small, g_b_near],
+        scratch=[(64, 512), (1, 512), (512, 512)],
+        copies=3,
         final=(0, 1, 2),
     )
     arr6 = swap(pay6, PATHS)

time: 140 us -> 140 us (level)
    pallas_call x10 -> x11, Pallas kernels: 16.4 us -> 16.6 us  [call(): pl.pallas_call(kernel, out_shape=shapes, in_specs=[smem] * len(scalars) +...]
where the time goes in v5:
time: 140 us; the launch traced here: 139 us
  blocking collectives  108 us (77%)
  Pallas kernels  16.6 us (12%)
  starting transfers between devices  12.2 us (9%)
  waiting for transfers between devices  1.59 us (1%)
    all_to_all x6, blocking collectives, swap(): return lax.all_to_all(x, axis, 0, 0, tiled=True)  108 us
    pallas_call x11, Pallas kernels, call(): pl.pallas_call(kernel, out_shape=shapes, in_specs=[smem] * len(scalars) +...  16.6 us
    ppermute x1, starting transfers between devices, on_device(): got = lax.ppermute(other, 'trades_1', [(0, 1), (1, 0)])  8.75 us
    ppermute x1, starting transfers between devices, on_device(): other = lax.ppermute(trunk, 'trades_1', [(0, 1), (1, 0)])  3.44 us
  transfers between devices with their start and end apart: 2, of which 2 were waited for; matrix products, arithmetic and copies ran while one was open for 0% of the time, Pallas kernels for 1%

profile of v5, /device:TPU:1, one launch (start us, length us, event | category | flops | bytes accessed | tf_op | source)
XLA Modules:
  0.0 139.5 jit_solution(11681361739638606923)
XLA Ops:
  0.6 4.1 %forward_kernel.1 = (f32[8,72,128]{2,1,0:T(8,128)S(1)}, f32[8,72,128]{2,1,0:T(8,128)S(1)}, f32[512,256]{1,0:T(8,128)S(1)}, f32[512,256]{1,0:T(8,128)S(1)}, f32[256,256]{1,0:T(8,128)S(1)}, /*index=5*/f32[8,512]{1,0:T(8,128)S(1)}) custom-call(s32[1]{0:T(128)} %bitcast.1.path.own, s32[1]{0:T(128)} %bitcast.2.trade.own, s32[1]{0:T(128)} %bitcast.core.own, ...), custom_call_target="tpu_custom_call" | custom-call | flops 1000000000 | tf_op jit(solution)/shard_map/forward_kernel/pallas_call | solution.py:335
  4.7 8.7 %collective-permute-start = (f32[8,72,128]{2,1,0:T(8,128)S(1)}, f32[8,72,128]{2,1,0:T(8,128)S(1)}, u32[]{:S(2)}, u32[]{:S(2)}) collective-permute-start(f32[8,72,128]{2,1,0:T(8,128)S(1)} %get-tuple-element.26), channel_id=1, source_target_pairs={{0,1},{1,0},{2,3},{3,2},{4,5},{5,4},{6,7},{7,6},{8,9},{9,8},{10,11... | collective-permute-start | bytes 884744 | tf_op jit(solution)/shard_map/ppermute | solution.py:377
  13.5 0.0 copy-start
  13.5 0.0 copy-start.2
  13.5 0.0 copy-start.3
  13.5 0.0 copy-start.4
  13.5 0.4 head_grad_kernel.1.g_head
  13.9 0.7 collective-permute-done.got
  14.7 15.0 %all_to_all.30.arrived = f32[8,72,128]{2,1,0:T(8,128)S(1)} all-to-all(f32[8,72,128]{2,1,0:T(8,128)S(1)} %join_kernel.1), channel_id=1, replica_groups=mesh['x'=4,'z'=8,'trades_0'=8,'trades_1'=2] {'trades_0'}, dimensions={0} | all-to-all | bytes 589824 | tf_op jit(solution)/shard_map/all_to_all | solution.py:350
  29.7 0.0 copy-done
  29.7 0.0 copy-done.2
  29.7 0.0 copy-done.3
  29.7 0.0 copy-done.4
  29.7 4.3 %backward_kernel.1 = f32[32,48,128]{2,1,0:T(8,128)S(1)} custom-call(s32[1]{0:T(128)} %bitcast.2.trade.own, f32[8,72,128]{2,1,0:T(8,128)S(1)} %all_to_all.30.arrived, f32[64,256]{1,0:T(8,128)S(1)} %bitcast.17, f32[64,256]{1,0:T(8,128)S(1)} %bitcast.18, f32[64,512]{1,0:T(8,128)S(1)} %copy-done.2, f32[512,512]{1,0:T(8,128)S(1)} %copy-done, ...), custom_call_target="tpu_custom_call" | custom-call | flops 1000000000 | tf_op jit(solution)/shard_map/backward_kernel/pallas_call | solution.py:335
  34.1 0.0 copy-start.1
  34.1 31.2 %all_to_all.31.arrived = f32[32,48,128]{2,1,0:T(8,128)S(1)} all-to-all(f32[32,48,128]{2,1,0:T(8,128)S(1)} %backward_kernel.1), channel_id=1, replica_groups=mesh['x'=4,'z'=8,'trades_0'=8,'trades_1'=2] {'x','z'}, dimensions={0} | all-to-all | bytes 1572864 | tf_op jit(solution)/shard_map/all_to_all | solution.py:350
  65.2 0.0 copy-done.1
  65.2 0.7 net_kernel.1
  65.9 16.0 %all_to_all.32.arrived = f32[16,16,128]{2,1,0:T(8,128)S(1)} all-to-all(f32[16,16,128]{2,1,0:T(8,128)S(1)} %get-tuple-element.33), channel_id=1, replica_groups=mesh['x'=4,'z'=8,'trades_0'=8,'trades_1'=2] {'trades_0','trades_1'}, dimensions={0} | all-to-all | bytes 262144 | tf_op jit(solution)/shard_map/all_to_all | solution.py:350
  81.9 0.7 gather_kernel.1
  82.7 16.1 %all_to_all.33.arrived = f32[8,72,128]{2,1,0:T(8,128)S(1)} all-to-all(f32[8,72,128]{2,1,0:T(8,128)S(1)} %get-tuple-element.35), channel_id=1, replica_groups=mesh['x'=4,'z'=8,'trades_0'=8,'trades_1'=2] {'z'}, dimensions={0} | all-to-all | bytes 589824 | tf_op jit(solution)/shard_map/all_to_all | solution.py:350
  98.7 0.1 spread_kernel.1
  98.8 18.5 %all_to_all.34 = f32[4,576,128]{2,1,0:T(8,128)S(1)} all-to-all(f32[4,576,128]{2,1,0:T(8,128)S(1)} %spread_kernel.1), channel_id=1, replica_groups=mesh['x'=4,'z'=8,'trades_0'=8,'trades_1'=2] {'x'}, dimensions={0} | all-to-all | bytes 2359296 | tf_op jit(solution)/shard_map/all_to_all | solution.py:350
  117.3 0.0 copy-start.5
  117.4 3.4 %collective-permute-start.1 = (f32[32,40,128]{2,1,0:T(8,128)S(1)}, f32[32,40,128]{2,1,0:T(8,128)S(1)}, u32[]{:S(2)}, u32[]{:S(2)}) collective-permute-start(f32[32,40,128]{2,1,0:T(8,128)S(1)} %trim_kernel.1.mine), channel_id=1, source_target_pairs={{0,1},{1,0},{2,3},{3,2},{4,5},{5,4},{6,7},{7,6},{8,9},{9,8},{10,11... | collective-permute-start | bytes 1966088 | tf_op jit(solution)/shard_map/ppermute | solution.py:421
  120.8 0.8 head_out_kernel.1
  121.6 0.9 collective-permute-done.1.other
  122.5 0.0 copy-done.5
  122.5 4.6 %infer_kernel.1 = (f32[64,512]{1,0:T(8,128)}, f32[1,512]{1,0:T(1,128)}, f32[512,512]{1,0:T(8,128)}, f32[32,1,128]{2,1,0:T(1,128)S(1)}) custom-call(s32[1]{0:T(128)} %bitcast.core.own, f32[32,40,128]{2,1,0:T(8,128)S(1)} %trim_kernel.1.mine, f32[32,40,128]{2,1,0:T(8,128)S(1)} %collective-permute-done.1.other, f32[64,512]{1,0:T(8,128)S(1)} %copy-done.2, ...), custom_call_target="tpu_custom_call" | custom-call | flops 1000000000 | tf_op jit(solution)/shard_map/infer_kernel/pallas_call | solution.py:335
  127.2 11.6 %all_to_all.35.lines = f32[32,1,128]{2,1,0:T(1,128)S(1)} all-to-all(f32[32,1,128]{2,1,0:T(1,128)S(1)} %get-tuple-element.43), channel_id=1, replica_groups=mesh['x'=4,'z'=8,'trades_0'=8,'trades_1'=2] {'x','z'}, dimensions={0} | all-to-all | bytes 32768 | tf_op jit(solution)/shard_map/all_to_all | solution.py:350
  138.8 0.7 finish_kernel.1
  (2 shorter events, 0.1 us)
Async XLA Ops:
  4.7 9.9 %collective-permute-start = (f32[8,72,128]{2,1,0:T(8,128)S(1)}, f32[8,72,128]{2,1,0:T(8,128)S(1)}, u32[]{:S(2)}, u32[]{:S(2)}) collective-permute-start(f32[8,72,128]{2,1,0:T(8,128)S(1)} %get-tuple-element.26), channel_id=1, source_target_pairs={{0,1},{1,0},{2,3},{3,2},{4,5},{5,4},{6,7},{7,6},{8,9},{9,8},{10,11... | collective-permute-start | bytes 884744 | tf_op jit(solution)/shard_map/ppermute | solution.py:377
  13.5 16.2 %copy-start = (f32[512,512]{1,0:T(8,128)S(1)}, f32[512,512]{1,0:T(8,128)}, u32[]{:S(2)}) copy-start(f32[512,512]{1,0:T(8,128)} %w_mid.5) | copy-start | bytes 3145732
  13.5 16.2 %copy-start.2 = (f32[64,512]{1,0:T(8,128)S(1)}, f32[64,512]{1,0:T(8,128)}, u32[]{:S(2)}) copy-start(f32[64,512]{1,0:T(8,128)} %w_in.5) | copy-start | bytes 393220
  13.5 16.2 %copy-start.3 = (f32[256,64]{0,1:T(8,128)S(1)}, f32[256,64]{0,1:T(8,128)}, u32[]{:S(2)}) copy-start(f32[256,64]{0,1:T(8,128)} %param.12) | copy-start | bytes 196612
  13.5 16.2 %copy-start.4 = (f32[256,64]{0,1:T(8,128)S(1)}, f32[256,64]{0,1:T(8,128)}, u32[]{:S(2)}) copy-start(f32[256,64]{0,1:T(8,128)} %param.14) | copy-start | bytes 196612
  34.1 31.2 %copy-start.1 = (f32[512,256]{1,0:T(8,128)S(1)}, f32[512,256]{1,0:T(8,128)}, u32[]{:S(2)}) copy-start(f32[512,256]{1,0:T(8,128)} %head.3) | copy-start | bytes 1572868
  117.3 5.2 %copy-start.5 = (f32[4,256,64]{1,2,0:T(8,128)S(1)}, f32[4,256,64]{1,2,0:T(8,128)}, u32[]{:S(2)}) copy-start(f32[4,256,64]{1,2,0:T(8,128)} %param.15) | copy-start | bytes 786436
  117.4 5.2 %collective-permute-start.1 = (f32[32,40,128]{2,1,0:T(8,128)S(1)}, f32[32,40,128]{2,1,0:T(8,128)S(1)}, u32[]{:S(2)}, u32[]{:S(2)}) collective-permute-start(f32[32,40,128]{2,1,0:T(8,128)S(1)} %trim_kernel.1.mine), channel_id=1, source_target_pairs={{0,1},{1,0},{2,3},{3,2},{4,5},{5,4},{6,7},{7,6},{8,9},{9,8},{10,11... | collective-permute-start | bytes 1966088 | tf_op jit(solution)/shard_map/ppermute | solution.py:421

commit v6 on v5

--- a/solution.py
+++ b/solution.py
@@ -292,14 +292,16 @@
     net_head = halves(both)
     row = jnp.zeros((1, 128), F32)
     lane = lane_index((1, 128))
+    x_rows = jnp.concatenate([x_t[d].T for d in range(4)], axis=0)
+    high, low = halves(x_rows)
+    first_pre = jnp.dot(
+        jnp.concatenate([high, low, high], axis=1), deep_in, preferred_element_type=F32
+    )
+    a1 = softplus(first_pre + new_b_in)
+    a2 = softplus(mm(halves(a1), new_mid) + new_b_mid)
+    netted = jnp.maximum(mm_narrow(halves(a2), net_head), 0.0)
     for d in range(4):
-        high, low = halves(x_t[d].T)
-        rows = jnp.concatenate([high, low, high], axis=1)
-        first_pre = jnp.dot(rows, deep_in, preferred_element_type=F32)
-        a1 = softplus(first_pre + new_b_in)
-        a2 = softplus(mm(halves(a1), new_mid) + new_b_mid)
-        netted = mm_narrow(halves(a2), net_head)
-        line = jnp.sum(jnp.maximum(netted, 0.0), axis=0, keepdims=True)
+        line = jnp.sum(netted[256 * d : 256 * d + 256], axis=0, keepdims=True)
         moved = pltpu.roll(line, (16 * d - LANE_NET) % 128, 1)
         row = jnp.where((lane >= 16 * d) & (lane < 16 * d + 16), moved, row)
     pay[...] = jnp.broadcast_to(row[None], (32, 1, 128))

time: 140 us -> 139 us (level)
  no operation moved by 1% of the time
where the time goes in v6:
time: 139 us
  blocking collectives  108 us (78%)
  Pallas kernels  15.9 us (11%)
  starting transfers between devices  12.2 us (9%)
  waiting for transfers between devices  1.59 us (1%)
    all_to_all x6, blocking collectives, swap(): return lax.all_to_all(x, axis, 0, 0, tiled=True)  108 us
    pallas_call x11, Pallas kernels, call(): pl.pallas_call(kernel, out_shape=shapes, in_specs=[smem] * len(scalars) +...  15.9 us
    ppermute x1, starting transfers between devices, on_device(): got = lax.ppermute(other, 'trades_1', [(0, 1), (1, 0)])  8.75 us
    ppermute x1, starting transfers between devices, on_device(): other = lax.ppermute(trunk, 'trades_1', [(0, 1), (1, 0)])  3.44 us
  transfers between devices with their start and end apart: 2, of which 2 were waited for; matrix products, arithmetic and copies ran while one was open for 0% of the time, Pallas kernels for 1%

profile of v6, /device:TPU:1, one launch (start us, length us, event | category | flops | bytes accessed | tf_op | source)
XLA Modules:
  0.0 138.9 jit_solution(15708002186337358573)
XLA Ops:
  0.6 4.1 %forward_kernel.1 = (f32[8,72,128]{2,1,0:T(8,128)S(1)}, f32[8,72,128]{2,1,0:T(8,128)S(1)}, f32[512,256]{1,0:T(8,128)S(1)}, f32[512,256]{1,0:T(8,128)S(1)}, f32[256,256]{1,0:T(8,128)S(1)}, /*index=5*/f32[8,512]{1,0:T(8,128)S(1)}) custom-call(s32[1]{0:T(128)} %bitcast.1.path.own, s32[1]{0:T(128)} %bitcast.2.trade.own, s32[1]{0:T(128)} %bitcast.core.own, ...), custom_call_target="tpu_custom_call" | custom-call | flops 1000000000 | tf_op jit(solution)/shard_map/forward_kernel/pallas_call | solution.py:337
  4.7 8.7 %collective-permute-start = (f32[8,72,128]{2,1,0:T(8,128)S(1)}, f32[8,72,128]{2,1,0:T(8,128)S(1)}, u32[]{:S(2)}, u32[]{:S(2)}) collective-permute-start(f32[8,72,128]{2,1,0:T(8,128)S(1)} %get-tuple-element.26), channel_id=1, source_target_pairs={{0,1},{1,0},{2,3},{3,2},{4,5},{5,4},{6,7},{7,6},{8,9},{9,8},{10,11... | collective-permute-start | bytes 884744 | tf_op jit(solution)/shard_map/ppermute | solution.py:379
  13.5 0.0 copy-start
  13.5 0.0 copy-start.2
  13.5 0.0 copy-start.3
  13.5 0.0 copy-start.4
  13.5 0.4 head_grad_kernel.1.g_head
  13.9 0.7 collective-permute-done.got
  14.7 15.0 %all_to_all.30.arrived = f32[8,72,128]{2,1,0:T(8,128)S(1)} all-to-all(f32[8,72,128]{2,1,0:T(8,128)S(1)} %join_kernel.1), channel_id=1, replica_groups=mesh['x'=4,'z'=8,'trades_0'=8,'trades_1'=2] {'trades_0'}, dimensions={0} | all-to-all | bytes 589824 | tf_op jit(solution)/shard_map/all_to_all | solution.py:352
  29.7 0.0 copy-done
  29.7 0.0 copy-done.2
  29.7 0.0 copy-done.3
  29.7 0.0 copy-done.4
  29.7 4.3 %backward_kernel.1 = f32[32,48,128]{2,1,0:T(8,128)S(1)} custom-call(s32[1]{0:T(128)} %bitcast.2.trade.own, f32[8,72,128]{2,1,0:T(8,128)S(1)} %all_to_all.30.arrived, f32[64,256]{1,0:T(8,128)S(1)} %bitcast.17, f32[64,256]{1,0:T(8,128)S(1)} %bitcast.18, f32[64,512]{1,0:T(8,128)S(1)} %copy-done.2, f32[512,512]{1,0:T(8,128)S(1)} %copy-done, ...), custom_call_target="tpu_custom_call" | custom-call | flops 1000000000 | tf_op jit(solution)/shard_map/backward_kernel/pallas_call | solution.py:337
  34.1 0.0 copy-start.1
  34.1 31.2 %all_to_all.31.arrived = f32[32,48,128]{2,1,0:T(8,128)S(1)} all-to-all(f32[32,48,128]{2,1,0:T(8,128)S(1)} %backward_kernel.1), channel_id=1, replica_groups=mesh['x'=4,'z'=8,'trades_0'=8,'trades_1'=2] {'x','z'}, dimensions={0} | all-to-all | bytes 1572864 | tf_op jit(solution)/shard_map/all_to_all | solution.py:352
  65.2 0.0 copy-done.1
  65.2 0.7 net_kernel.1
  65.9 16.0 %all_to_all.32.arrived = f32[16,16,128]{2,1,0:T(8,128)S(1)} all-to-all(f32[16,16,128]{2,1,0:T(8,128)S(1)} %get-tuple-element.33), channel_id=1, replica_groups=mesh['x'=4,'z'=8,'trades_0'=8,'trades_1'=2] {'trades_0','trades_1'}, dimensions={0} | all-to-all | bytes 262144 | tf_op jit(solution)/shard_map/all_to_all | solution.py:352
  81.9 0.7 gather_kernel.1
  82.7 16.1 %all_to_all.33.arrived = f32[8,72,128]{2,1,0:T(8,128)S(1)} all-to-all(f32[8,72,128]{2,1,0:T(8,128)S(1)} %get-tuple-element.35), channel_id=1, replica_groups=mesh['x'=4,'z'=8,'trades_0'=8,'trades_1'=2] {'z'}, dimensions={0} | all-to-all | bytes 589824 | tf_op jit(solution)/shard_map/all_to_all | solution.py:352
  98.7 0.1 spread_kernel.1
  98.8 18.5 %all_to_all.34 = f32[4,576,128]{2,1,0:T(8,128)S(1)} all-to-all(f32[4,576,128]{2,1,0:T(8,128)S(1)} %spread_kernel.1), channel_id=1, replica_groups=mesh['x'=4,'z'=8,'trades_0'=8,'trades_1'=2] {'x'}, dimensions={0} | all-to-all | bytes 2359296 | tf_op jit(solution)/shard_map/all_to_all | solution.py:352
  117.3 0.0 copy-start.5
  117.4 3.4 %collective-permute-start.1 = (f32[32,40,128]{2,1,0:T(8,128)S(1)}, f32[32,40,128]{2,1,0:T(8,128)S(1)}, u32[]{:S(2)}, u32[]{:S(2)}) collective-permute-start(f32[32,40,128]{2,1,0:T(8,128)S(1)} %trim_kernel.1.mine), channel_id=1, source_target_pairs={{0,1},{1,0},{2,3},{3,2},{4,5},{5,4},{6,7},{7,6},{8,9},{9,8},{10,11... | collective-permute-start | bytes 1966088 | tf_op jit(solution)/shard_map/ppermute | solution.py:423
  120.8 0.8 head_out_kernel.1
  121.6 0.9 collective-permute-done.1.other
  122.5 0.0 copy-done.5
  122.5 4.0 %infer_kernel.1 = (f32[64,512]{1,0:T(8,128)}, f32[1,512]{1,0:T(1,128)}, f32[512,512]{1,0:T(8,128)}, f32[32,1,128]{2,1,0:T(1,128)S(1)}) custom-call(s32[1]{0:T(128)} %bitcast.core.own, f32[32,40,128]{2,1,0:T(8,128)S(1)} %trim_kernel.1.mine, f32[32,40,128]{2,1,0:T(8,128)S(1)} %collective-permute-done.1.other, f32[64,512]{1,0:T(8,128)S(1)} %copy-done.2, ...), custom_call_target="tpu_custom_call" | custom-call | flops 1000000000 | tf_op jit(solution)/shard_map/infer_kernel/pallas_call | solution.py:337
  126.5 11.6 %all_to_all.35.lines = f32[32,1,128]{2,1,0:T(1,128)S(1)} all-to-all(f32[32,1,128]{2,1,0:T(1,128)S(1)} %get-tuple-element.43), channel_id=1, replica_groups=mesh['x'=4,'z'=8,'trades_0'=8,'trades_1'=2] {'x','z'}, dimensions={0} | all-to-all | bytes 32768 | tf_op jit(solution)/shard_map/all_to_all | solution.py:352
  138.2 0.7 finish_kernel.1
  (2 shorter events, 0.1 us)
Async XLA Ops:
  4.7 9.9 %collective-permute-start = (f32[8,72,128]{2,1,0:T(8,128)S(1)}, f32[8,72,128]{2,1,0:T(8,128)S(1)}, u32[]{:S(2)}, u32[]{:S(2)}) collective-permute-start(f32[8,72,128]{2,1,0:T(8,128)S(1)} %get-tuple-element.26), channel_id=1, source_target_pairs={{0,1},{1,0},{2,3},{3,2},{4,5},{5,4},{6,7},{7,6},{8,9},{9,8},{10,11... | collective-permute-start | bytes 884744 | tf_op jit(solution)/shard_map/ppermute | solution.py:379
  13.5 16.2 %copy-start = (f32[512,512]{1,0:T(8,128)S(1)}, f32[512,512]{1,0:T(8,128)}, u32[]{:S(2)}) copy-start(f32[512,512]{1,0:T(8,128)} %w_mid.5) | copy-start | bytes 3145732
  13.5 16.2 %copy-start.2 = (f32[64,512]{1,0:T(8,128)S(1)}, f32[64,512]{1,0:T(8,128)}, u32[]{:S(2)}) copy-start(f32[64,512]{1,0:T(8,128)} %w_in.5) | copy-start | bytes 393220
  13.5 16.2 %copy-start.3 = (f32[256,64]{0,1:T(8,128)S(1)}, f32[256,64]{0,1:T(8,128)}, u32[]{:S(2)}) copy-start(f32[256,64]{0,1:T(8,128)} %param.12) | copy-start | bytes 196612
  13.5 16.2 %copy-start.4 = (f32[256,64]{0,1:T(8,128)S(1)}, f32[256,64]{0,1:T(8,128)}, u32[]{:S(2)}) copy-start(f32[256,64]{0,1:T(8,128)} %param.14) | copy-start | bytes 196612
  34.1 31.2 %copy-start.1 = (f32[512,256]{1,0:T(8,128)S(1)}, f32[512,256]{1,0:T(8,128)}, u32[]{:S(2)}) copy-start(f32[512,256]{1,0:T(8,128)} %head.3) | copy-start | bytes 1572868
  117.3 5.2 %copy-start.5 = (f32[4,256,64]{1,2,0:T(8,128)S(1)}, f32[4,256,64]{1,2,0:T(8,128)}, u32[]{:S(2)}) copy-start(f32[4,256,64]{1,2,0:T(8,128)} %param.15) | copy-start | bytes 786436
  117.4 5.2 %collective-permute-start.1 = (f32[32,40,128]{2,1,0:T(8,128)S(1)}, f32[32,40,128]{2,1,0:T(8,128)S(1)}, u32[]{:S(2)}, u32[]{:S(2)}) collective-permute-start(f32[32,40,128]{2,1,0:T(8,128)S(1)} %trim_kernel.1.mine), channel_id=1, source_target_pairs={{0,1},{1,0},{2,3},{3,2},{4,5},{5,4},{6,7},{7,6},{8,9},{9,8},{10,11... | collective-permute-start | bytes 1966088 | tf_op jit(solution)/shard_map/ppermute | solution.py:423
